TPU v7x, 32 devices: a whole 2x2x4 slice. The times are simulated.
32 devices in a mesh: rows: 32 (over z, y, x, core).
Axes of the slice: x: 2, y: 2, z: 4, core: 2. Of those that a mesh axis runs over, the one named last changes fastest.
Arguments:
- source: float32 [64, 131072], P(None, 'rows'), may hold values from -6 to 6
- band_values: float32 [128, 131072], P(None, 'rows'), may hold values from -0.625 to 0.625
- offsets: int32 [128], replicated, may hold values from -128 to 128, as said below
Outputs:
- compressed: float32 [128, 131072], P(None, 'rows')
Inputs may be any that keep to these rules, and one draw needn't show every extreme that they name: The 128 offsets are distinct and include both -128 and 128.
All inputs are finite; a program needn't handle non-finite values.
Results may differ from a plain program's by a relative error of at most 0.0003.
Values sent between devices are 32-bit elements; how exact they have to be, the bound alone decides.
A program may use at most 192 MiB of HBM per device.

v0:
```python
import functools

import jax
import jax.numpy as jnp
from jax import lax
from jax.experimental import pallas as pl
from jax.experimental.pallas import tpu as pltpu
from jax.sharding import PartitionSpec as P

HB = 128
K2 = 128
SUB = 8
LANE = 128
MESH = pl.DeviceIdType.MESH
VMEM = pl.BlockSpec(memory_space=pltpu.VMEM)
HBM = pl.BlockSpec(memory_space=pltpu.HBM)
NT = (((1,), (1,)), ((), ()))


def exact(a, b, dims=(((1,), (0,)), ((), ()))):
    return lax.dot_general(
        a, b, dims, precision=lax.Precision.HIGHEST, preferred_element_type=jnp.float32
    )


def bf(a, b, dims=(((1,), (0,)), ((), ()))):
    return lax.dot_general(a, b, dims, preferred_element_type=jnp.float32)


def halves(value):
    high = value.astype(jnp.bfloat16)
    low = (value - high.astype(jnp.float32)).astype(jnp.bfloat16)
    return high, low


def halo_kernel(n, source, band, low_s, high_s, low_b, high_b, ls, hs, lb, hb, send, recv):
    me = lax.axis_index("rows")
    right, left = lax.rem(me + 1, n), lax.rem(me + n - 1, n)
    barrier = pltpu.get_barrier_semaphore()
    for neighbour in (left, right):
        pl.semaphore_signal(barrier, inc=1, device_id=(neighbour,), device_id_type=MESH)
    pl.semaphore_wait(barrier, 2)
    local = source.shape[1]
    deep_s, deep_b = ls.shape[1], lb.shape[1]
    moves = (
        (band.at[:, pl.ds(local - deep_b, deep_b)], lb, right),
        (band.at[:, pl.ds(0, deep_b)], hb, left),
        (source.at[:, pl.ds(local - deep_s, deep_s)], ls, right),
        (source.at[:, pl.ds(0, deep_s)], hs, left),
    )
    copies = []
    for index, (src, dst, target) in enumerate(moves):
        copies.append(
            pltpu.make_async_remote_copy(
                src_ref=src,
                dst_ref=dst,
                send_sem=send.at[index],
                recv_sem=recv.at[index],
                device_id=(target,),
                device_id_type=MESH,
            )
        )
    for copy in copies:
        copy.start()
    for copy in copies:
        copy.wait()
    low_b[...] = jnp.where(me > 0, lb[...], 0.0)
    high_b[...] = jnp.where(me < n - 1, hb[...], 0.0)
    low_s[...] = jnp.where(me > 0, ls[...], 0.0)
    high_s[...] = jnp.where(me < n - 1, hs[...], 0.0)


def halos(source, band):
    n = lax.axis_size("rows")
    shapes = [(source.shape[0], 3 * HB)] * 2 + [(band.shape[0], 2 * HB)] * 2
    return pl.pallas_call(
        functools.partial(halo_kernel, n),
        out_shape=[jax.ShapeDtypeStruct(shape, jnp.float32) for shape in shapes],
        in_specs=[HBM] * 2,
        out_specs=[VMEM] * 4,
        scratch_shapes=[pltpu.VMEM(shape, jnp.float32) for shape in shapes]
        + [pltpu.SemaphoreType.DMA((4,)), pltpu.SemaphoreType.DMA((4,))],
        compiler_params=pltpu.CompilerParams(
            collective_id=0, has_side_effects=True, vmem_limit_bytes=8 << 20
        ),
    )(source, band)


def total_kernel(n, owners, g, out, got, total, gathered, s1, r1, s2, r2):
    me = lax.axis_index("rows")
    stride = n // owners
    mine = me // stride
    barrier = pltpu.get_barrier_semaphore()

    def greet(k, _):
        pl.semaphore_signal(
            barrier, inc=1, device_id=(lax.rem(me + k, n),), device_id_type=MESH
        )
        return 0

    lax.fori_loop(1, n, greet, 0)
    pl.semaphore_wait(barrier, n - 1)

    def outward(o):
        return pltpu.make_async_remote_copy(
            src_ref=g.at[o],
            dst_ref=got.at[me],
            send_sem=s1.at[o],
            recv_sem=r1.at[me],
            device_id=(o * stride,),
            device_id_type=MESH,
        )

    def inward(other):
        return pltpu.make_async_remote_copy(
            src_ref=g.at[0],
            dst_ref=got.at[other],
            send_sem=s1.at[0],
            recv_sem=r1.at[other],
            device_id=(other,),
            device_id_type=MESH,
        )

    def back(other):
        return pltpu.make_async_remote_copy(
            src_ref=total,
            dst_ref=gathered.at[mine],
            send_sem=s2.at[other],
            recv_sem=r2.at[mine],
            device_id=(other,),
            device_id_type=MESH,
        )

    def spread(o):
        return pltpu.make_async_remote_copy(
            src_ref=total,
            dst_ref=gathered.at[o],
            send_sem=s2.at[0],
            recv_sem=r2.at[o],
            device_id=(o * stride,),
            device_id_type=MESH,
        )

    def send_out(k, _):
        o = lax.rem(mine + k, owners)

        @pl.when(o * stride != me)
        def _():
            outward(o).start()

        return 0

    lax.fori_loop(0, owners, send_out, 0)

    @pl.when(mine * stride == me)
    def _():
        got[me] = g[mine]

        def arrive(k, _):
            inward(lax.rem(me + k, n)).wait_recv()
            return 0

        lax.fori_loop(1, n, arrive, 0)
        summed = jnp.sum(got[...], axis=0)
        total[...] = summed
        gathered[mine] = summed

        def send_back(k, _):
            back(lax.rem(me + k, n)).start()
            return 0

        lax.fori_loop(1, n, send_back, 0)

    def collect(o, _):
        @pl.when(o * stride != me)
        def _():
            spread(o).wait_recv()
            outward(o).wait_send()

        return 0

    lax.fori_loop(0, owners, collect, 0)
    out[...] = gathered[...]

    @pl.when(mine * stride == me)
    def _():
        def sent(k, _):
            back(lax.rem(me + k, n)).wait_send()
            return 0

        lax.fori_loop(1, n, sent, 0)


def all_total(value, ident):
    n = lax.axis_size("rows")
    rows, columns = value.shape
    owners = rows // SUB
    shape = (owners, SUB, columns)
    dma = pltpu.SemaphoreType.DMA
    summed = pl.pallas_call(
        functools.partial(total_kernel, n, owners),
        out_shape=jax.ShapeDtypeStruct(shape, jnp.float32),
        in_specs=[VMEM],
        out_specs=VMEM,
        scratch_shapes=[
            pltpu.VMEM((n, SUB, columns), jnp.float32),
            pltpu.VMEM((SUB, columns), jnp.float32),
            pltpu.VMEM(shape, jnp.float32),
            dma((owners,)),
            dma((n,)),
            dma((n,)),
            dma((owners,)),
        ],
        compiler_params=pltpu.CompilerParams(
            collective_id=ident, has_side_effects=True, vmem_limit_bytes=8 << 20
        ),
    )(value.reshape(shape))
    return summed.reshape(rows, columns)


def banded(window_high, window_low, band_high, band_low):
    return (
        bf(window_high, band_high, NT)
        + bf(window_low, band_high, NT)
        + bf(window_high, band_low, NT)
    )


def squares(high, low):
    mixed = bf(high, low, NT)
    return bf(high, high, NT) + mixed + mixed.T


def columns_of(block, count=1):
    return pl.ds(pl.multiple_of(block * HB, HB), count * HB)


def first_kernel(
    source, band, offsets, low_s, high_s, low_b, high_b,
    first, upper, lower, gram, high, low, values
):
    width, local = source.shape
    blocks = upper.shape[0]
    for piece, at in ((low_s, 0), (source, 3 * HB), (high_s, 3 * HB + local)):
        part = piece[...]
        where = pl.ds(at, part.shape[1])
        top, bottom = halves(part)
        high[:, where] = top
        low[:, where] = bottom
    first[:width, pl.ds(0, 2 * HB)] = low_s[:, pl.ds(HB, 2 * HB)]
    first[:width, pl.ds(2 * HB, local)] = source[...]
    first[:width, pl.ds(2 * HB + local, 2 * HB)] = high_s[:, pl.ds(0, 2 * HB)]
    values[:, pl.ds(0, 2 * HB)] = low_b[...]
    values[:, pl.ds(2 * HB, local)] = band[...]
    values[:, pl.ds(2 * HB + local, 2 * HB)] = high_b[...]
    diagonals = band.shape[0]
    places = lax.broadcasted_iota(jnp.int32, (diagonals, 3 * HB), 1)
    chosen = jnp.where(places == offsets[...] + HB, 1.0, 0.0).astype(jnp.bfloat16)
    chosen = jnp.concatenate([chosen, chosen], axis=0)

    def step(block, _):
        top, bottom = halves(values[:, columns_of(block)].T)
        spread = bf(jnp.concatenate([top, bottom], axis=1), chosen)
        sheared = pltpu.roll(spread, 0, 1, stride=1, stride_axis=0)
        band_high, band_low = halves(sheared)
        upper[block] = band_high
        lower[block] = band_low
        window = columns_of(block, 3)
        first[width:, columns_of(block)] = banded(
            high[:, window], low[:, window], band_high, band_low
        )
        return 0

    lax.fori_loop(0, blocks, step, 0, unroll=4)
    inner = first[:, pl.ds(2 * HB, local)]
    gram[...] = squares(*halves(inner))


def make_first(source, band, offsets, edges):
    width, local = source.shape
    diagonals = band.shape[0]
    deep = local + 4 * HB
    blocks = deep // HB
    return pl.pallas_call(
        first_kernel,
        out_shape=[
            jax.ShapeDtypeStruct((2 * width, deep), jnp.float32),
            jax.ShapeDtypeStruct((blocks, HB, 3 * HB), jnp.bfloat16),
            jax.ShapeDtypeStruct((blocks, HB, 3 * HB), jnp.bfloat16),
            jax.ShapeDtypeStruct((2 * width, 2 * width), jnp.float32),
        ],
        in_specs=[VMEM] * 7,
        out_specs=[VMEM] * 4,
        scratch_shapes=[
            pltpu.VMEM((width, deep + 2 * HB), jnp.bfloat16),
            pltpu.VMEM((width, deep + 2 * HB), jnp.bfloat16),
            pltpu.VMEM((diagonals, deep), jnp.float32),
        ],
        compiler_params=pltpu.CompilerParams(vmem_limit_bytes=28 << 20),
    )(source, band, offsets.reshape(diagonals, 1), *edges)


def splat(value):
    return jnp.broadcast_to(value, (SUB, LANE))


def eliminate(metric, right):
    tiles = metric.shape[0] // SUB
    part = [slice(SUB * t, SUB * t + SUB) for t in range(tiles)]
    state = [[metric[part[t]], right[part[t]]] for t in range(tiles)]
    rows = lax.broadcasted_iota(jnp.int32, (SUB, LANE), 0)
    solved = []
    steps = range(SUB)
    for t0 in range(tiles):
        at = SUB * t0
        core = {
            (i, k): splat(state[t0][0][i : i + 1, at + k : at + k + 1])
            for i in steps
            for k in range(i, SUB)
        }
        pivots = [[splat(half[i : i + 1]) for half in state[t0]] for i in steps]
        inverse = []
        for i in steps:
            inverse.append(1.0 / core[i, i])
            for k in range(i + 1, SUB):
                ratio = core[i, k] * inverse[i]
                for m in range(k, SUB):
                    core[k, m] = core[k, m] - ratio * core[i, m]
                pivots[k] = [p - ratio * q for p, q in zip(pivots[k], pivots[i])]
        result = jnp.zeros((SUB, LANE), jnp.float32)
        for i in steps:
            result = jnp.where(rows == i, pivots[i][1] * lax.rsqrt(core[i, i]), result)
        solved.append(result)
        for t in range(t0 + 1, tiles):
            scaled = []
            for k in steps:
                column = splat(state[t][0][:, at + k : at + k + 1])
                for i in range(k):
                    column = column - scaled[i] * core[i, k]
                scaled.append(column * inverse[k])
            for half in range(2):
                value = state[t][half]
                for k in steps:
                    value = value - scaled[k] * pivots[k][half]
                state[t][half] = value
    return jnp.concatenate(solved, axis=0)


def compress(grammian, retain):
    spanning = grammian[:retain]
    wide = spanning.shape[1] > retain
    across = lax.broadcasted_iota(jnp.int32, (retain, retain), 1)
    down = lax.broadcasted_iota(jnp.int32, (retain, retain), 0)
    unit = jnp.where(across == down, 1.0, 0.0)
    coeffs = None
    for repeat in range(2):
        if repeat > 0:
            spanning = exact(coeffs, grammian)
        metric = exact(exact(spanning, grammian), spanning, NT)
        metric = 0.5 * (metric + metric.T)
        if wide:
            coeffs = exact(eliminate(metric, unit), spanning)
        else:
            coeffs = eliminate(metric, spanning)
    return coeffs


def second_kernel(
    total, summed, first, upper, lower, factor, squared, corner, gram,
    high, low, once_high, once_low
):
    gram_one = summed[...] * (1.0 / total)
    keep = gram_one.shape[0]
    coeffs = compress(gram_one, keep)
    corner[...] = exact(exact(coeffs, gram_one), coeffs, NT)
    blocks = upper.shape[0]
    local = factor.shape[1]
    width = 4 * HB

    def expand(at, _):
        where = pl.ds(pl.multiple_of(at * width, width), width)
        top, bottom = halves(exact(coeffs, first[:, where]))
        high[:, where] = top
        low[:, where] = bottom
        return 0

    lax.fori_loop(0, first.shape[1] // width, expand, 0)

    def once(block, _):
        window = columns_of(block, 3)
        top, bottom = halves(
            banded(high[:, window], low[:, window], upper[block + 1], lower[block + 1])
        )
        once_high[:, columns_of(block)] = top
        once_low[:, columns_of(block)] = bottom
        return 0

    lax.fori_loop(0, blocks - 2, once, 0, unroll=4)

    def twice(block, _):
        window = columns_of(block, 3)
        squared[:, columns_of(block)] = banded(
            once_high[:, window], once_low[:, window], upper[block + 2], lower[block + 2]
        )
        return 0

    lax.fori_loop(0, blocks - 4, twice, 0, unroll=4)
    middle = pl.ds(2 * HB, local)
    factor[...] = high[:, middle].astype(jnp.float32) + low[:, middle].astype(jnp.float32)
    top, bottom = halves(squared[...])
    gram[:keep] = banded(high[:, middle], low[:, middle], top, bottom)
    gram[keep:] = squares(top, bottom)


def make_second(summed, first, upper, lower, total):
    keep, deep = first.shape
    local = deep - 4 * HB
    shape = jax.ShapeDtypeStruct
    return pl.pallas_call(
        functools.partial(second_kernel, total),
        out_shape=[
            shape((keep, local), jnp.float32),
            shape((keep, local), jnp.float32),
            shape((keep, keep), jnp.float32),
            shape((2 * keep, keep), jnp.float32),
        ],
        in_specs=[VMEM] * 4,
        out_specs=[VMEM] * 4,
        scratch_shapes=[
            pltpu.VMEM((keep, deep), jnp.bfloat16),
            pltpu.VMEM((keep, deep), jnp.bfloat16),
            pltpu.VMEM((keep, deep - 2 * HB), jnp.bfloat16),
            pltpu.VMEM((keep, deep - 2 * HB), jnp.bfloat16),
        ],
        compiler_params=pltpu.CompilerParams(vmem_limit_bytes=28 << 20),
    )(summed, first, upper, lower)


def last_kernel(total, summed, corner, factor, squared, out):
    keep = corner.shape[0]
    cross = summed[:keep] * (1.0 / total)
    own = summed[keep:] * (1.0 / total)
    top = jnp.concatenate([corner[...], cross], axis=1)
    bottom = jnp.concatenate([cross.T, own], axis=1)
    coeffs = compress(jnp.concatenate([top, bottom], axis=0), K2)
    width = 4 * HB

    def step(at, _):
        where = pl.ds(pl.multiple_of(at * width, width), width)
        stacked = jnp.concatenate([factor[:, where], squared[:, where]], axis=0)
        out[:, where] = exact(coeffs, stacked)
        return 0

    lax.fori_loop(0, out.shape[1] // width, step, 0)


def make_last(summed, corner, factor, squared, total):
    return pl.pallas_call(
        functools.partial(last_kernel, total),
        out_shape=jax.ShapeDtypeStruct((K2, factor.shape[1]), jnp.float32),
        in_specs=[VMEM] * 4,
        out_specs=VMEM,
        compiler_params=pltpu.CompilerParams(vmem_limit_bytes=28 << 20),
    )(summed, corner, factor, squared)


def body(source, band_values, offsets):
    total = float(source.shape[1] * lax.axis_size("rows"))
    edges = halos(source, band_values)
    first, upper, lower, gram = make_first(source, band_values, offsets, edges)
    summed = all_total(gram, 1)
    factor, squared, corner, gram = make_second(summed, first, upper, lower, total)
    summed = all_total(gram, 2)
    return make_last(summed, corner, factor, squared, total)


def solution(mesh):
    placed = (P(None, "rows"), P(None, "rows"), P())
    return jax.shard_map(
        body, mesh=mesh, in_specs=placed, out_specs=P(None, "rows"), check_vma=False
    )
```

profile of v0, /device:TPU:0, one launch (start us, length us, event | category | flops | bytes accessed | tf_op | source)
XLA Modules:
  0.0 104.3 jit_solution(16007661212151630450)
XLA Ops:
  0.0 0.8 copy.4.offsets
  0.8 0.0 copy-start
  0.8 1.6 %copy-done = f32[128,4096]{1,0:T(8,128)S(1)} copy-done((f32[128,4096]{1,0:T(8,128)S(1)}, f32[128,4096]{1,0:T(8,128)}, u32[]{:S(2)}) %copy-start) | copy-done | bytes 2097176
  2.4 0.0 copy-start.2
  2.4 1.2 %copy-done.2 = f32[64,4096]{1,0:T(8,128)S(1)} copy-done((f32[64,4096]{1,0:T(8,128)S(1)}, f32[64,4096]{1,0:T(8,128)}, u32[]{:S(2)}) %copy-start.2) | copy-done | bytes 1048600
  3.6 0.0 copy-start.1
  3.6 0.0 copy-start.3
  3.6 10.9 %shard_map.37 = (f32[64,384]{1,0:T(8,128)S(1)}, f32[64,384]{1,0:T(8,128)S(1)}, f32[128,256]{1,0:T(8,128)S(1)}, f32[128,256]{1,0:T(8,128)S(1)}) custom-call(f32[64,4096]{1,0:T(8,128)S(1)} %copy-done.2, f32[128,4096]{1,0:T(8,128)S(1)} %copy-done), custom_call_target="tpu_custom_call" | custom-call | tf_op jit(solution)/shard_map/pallas_call | solution.py:76
  14.5 0.0 copy-done.1
  14.5 0.0 copy-done.3
  14.5 17.0 %shard_map.38 = (f32[128,4608]{1,0:T(8,128)S(1)}, bf16[36,128,384]{2,1,0:T(8,128)(2,1)S(1)}, bf16[36,128,384]{2,1,0:T(8,128)(2,1)S(1)}, f32[128,128]{1,0:T(8,128)S(1)}) custom-call(f32[64,4096]{1,0:T(8,128)S(1)} %copy-done.3, f32[128,4096]{1,0:T(8,128)S(1)} %copy-done.1, s32[128,1]{1,0:T(8,128)S(1)} %copy.4.offsets, f32[64,384]{1,0:T(8,128)S(1)} %get-tuple-element.17.low_s, ...), custom_call_target="tpu_custom_call" | custom-call | tf_op jit(solution)/shard_map/pallas_call | solution.py:284
  31.5 15.5 %shard_map.39 = f32[16,8,128]{2,1,0:T(8,128)S(1)} custom-call(f32[16,8,128]{2,1,0:T(8,128)S(1)} %bitcast.8), custom_call_target="tpu_custom_call" | custom-call | tf_op jit(solution)/shard_map/pallas_call | solution.py:200
  47.0 26.9 %shard_map.40 = (f32[128,4096]{1,0:T(8,128)S(1)}, f32[128,4096]{1,0:T(8,128)S(1)}, f32[128,128]{1,0:T(8,128)S(1)}, f32[256,128]{1,0:T(8,128)S(1)}) custom-call(f32[128,128]{1,0:T(8,128)S(1)} %bitcast.6, f32[128,4608]{1,0:T(8,128)S(1)} %get-tuple-element.22.first, bf16[36,128,384]{2,1,0:T(8,128)(2,1)S(1)} %get-tuple-element.23.upper, ...), custom_call_target="tpu_custom_call" | custom-call | tf_op jit(solution)/shard_map/pallas_call | solution.py:419
  73.9 14.2 %shard_map.41 = f32[32,8,128]{2,1,0:T(8,128)S(1)} custom-call(f32[32,8,128]{2,1,0:T(8,128)S(1)} %bitcast.7), custom_call_target="tpu_custom_call" | custom-call | tf_op jit(solution)/shard_map/pallas_call | solution.py:200
  88.2 16.1 %shard_map.42 = f32[128,4096]{1,0:T(8,128)} custom-call(f32[256,128]{1,0:T(8,128)S(1)} %bitcast.5, f32[128,128]{1,0:T(8,128)S(1)} %get-tuple-element.26.corner, f32[128,4096]{1,0:T(8,128)S(1)} %get-tuple-element.27.factor, f32[128,4096]{1,0:T(8,128)S(1)} %get-tuple-element.28.squared), custom_call_target="tpu_custom_call" | custom-call | tf_op jit(solution)/shard_map/pallas_call | solution.py:458
Async XLA Ops:
  0.8 1.6 %copy-start = (f32[128,4096]{1,0:T(8,128)S(1)}, f32[128,4096]{1,0:T(8,128)}, u32[]{:S(2)}) copy-start(f32[128,4096]{1,0:T(8,128)} %band.3) | copy-start | bytes 6291460
  2.4 1.2 %copy-start.2 = (f32[64,4096]{1,0:T(8,128)S(1)}, f32[64,4096]{1,0:T(8,128)}, u32[]{:S(2)}) copy-start(f32[64,4096]{1,0:T(8,128)} %source.3) | copy-start | bytes 3145732
  3.6 10.9 %copy-start.1 = (f32[128,4096]{1,0:T(8,128)S(1)}, f32[128,4096]{1,0:T(8,128)}, u32[]{:S(2)}) copy-start(f32[128,4096]{1,0:T(8,128)} %band.3) | copy-start | bytes 6291460
  3.6 10.9 %copy-start.3 = (f32[64,4096]{1,0:T(8,128)S(1)}, f32[64,4096]{1,0:T(8,128)}, u32[]{:S(2)}) copy-start(f32[64,4096]{1,0:T(8,128)} %source.3) | copy-start | bytes 3145732
where the time goes:
time: 104 us
  Pallas kernels  101 us (97%)
  local copies, waits for them, and re-layouts  3.58 us (3%)
    pallas_call x2, Pallas kernels, all_total(): pl.pallas_call(functools.partial(total_kernel, n, owners), out_shape=jax....  29.7 us
    pallas_call x1, Pallas kernels, make_second(): pl.pallas_call(functools.partial(second_kernel, total), out_shape=[shape(...  26.9 us
    pallas_call x1, Pallas kernels, make_first(): pl.pallas_call(first_kernel, out_shape=[jax.ShapeDtypeStruct((2 * width,...  17 us
    pallas_call x1, Pallas kernels, make_last(): pl.pallas_call(functools.partial(last_kernel, total), out_shape=jax.Shape...  16.1 us
    pallas_call x1, Pallas kernels, halos(): pl.pallas_call(functools.partial(halo_kernel, n), out_shape=[jax.ShapeDty...  10.9 us
    unnamed x8, local copies, waits for them, and re-layouts  2.82 us

commit v1 on v0

v1 whole, which is shorter than its diff:
```python
import functools

import jax
import jax.numpy as jnp
from jax import lax
from jax.experimental import pallas as pl
from jax.experimental.pallas import tpu as pltpu
from jax.sharding import PartitionSpec as P

HB = 128
SUB = 8
LANE = 128
GROUP = 8
MESH = pl.DeviceIdType.MESH
VMEM = pl.BlockSpec(memory_space=pltpu.VMEM)
HBM = pl.BlockSpec(memory_space=pltpu.HBM)
NN = (((1,), (0,)), ((), ()))
NT = (((1,), (1,)), ((), ()))
TN = (((0,), (0,)), ((), ()))
F32 = jnp.float32
BF16 = jnp.bfloat16


def exact(a, b, dims=NN):
    return lax.dot_general(
        a, b, dims, precision=lax.Precision.HIGHEST, preferred_element_type=F32
    )


def bf(a, b, dims=NN):
    return lax.dot_general(a, b, dims, preferred_element_type=F32)


def halves(value):
    high = value.astype(BF16)
    low = (value - high.astype(F32)).astype(BF16)
    return high, low


def block(at, count=1):
    return pl.ds(pl.multiple_of(at * HB, HB), count * HB)


def pack(twice):
    lanes = lax.broadcasted_iota(jnp.int32, twice.shape, 1)
    high = twice.astype(BF16).astype(F32)
    return jnp.where(lanes < LANE // 2, high, twice - high).astype(BF16)


def pack_columns(part):
    return pack(jnp.concatenate([part, part], axis=0).T)


def band_block(values, chosen):
    top, bottom = halves(values.T)
    spread = bf(jnp.concatenate([top, bottom], axis=1), chosen)
    sheared = pltpu.roll(spread, 0, 1, stride=1, stride_axis=0)
    return jnp.concatenate(halves(sheared), axis=1)


def apply_block(bands, z, at):
    window = z[block(at, 3)]
    both = bf(bands[at], jnp.concatenate([window, window], axis=0))
    return pack(both + pltpu.roll(both, LANE // 2, 1))


def fold(square):
    half = LANE // 2
    rows = []
    for i in range(square.shape[0] // LANE):
        row = []
        for k in range(square.shape[1] // LANE):
            part = square[i * LANE : (i + 1) * LANE, k * LANE : (k + 1) * LANE]
            part = part[:half] + part[half:]
            row.append(part[:, :half] + part[:, half:])
        rows.append(jnp.concatenate(row, axis=1))
    return jnp.concatenate(rows, axis=0)


def main_kernel(
    n, source, band, offsets,
    z0, z1, z2, z3, gram,
    sv, bv, ls, hs, lb, hb, bands, mine, got, part, gotb, gathered,
    local_sem, hsend, hrecv, asend, arecv, bsend, brecv, csend, crecv,
):
    me = lax.axis_index("rows")
    right, left = lax.rem(me + 1, n), lax.rem(me + n - 1, n)
    groups = n // GROUP
    team, seat = me // GROUP, lax.rem(me, GROUP)
    local = source.shape[1]
    blocks = local // HB
    deep_s, deep_b = 3 * HB, 2 * HB

    def mate(k):
        return team * GROUP + lax.rem(seat + k, GROUP)

    def peer(k):
        return lax.rem(team + k, groups) * GROUP + seat

    barrier = pltpu.get_barrier_semaphore()

    def greet(device):
        pl.semaphore_signal(barrier, inc=1, device_id=(device,), device_id_type=MESH)

    greet(left)
    greet(right)
    for k in range(1, GROUP):
        greet(mate(k))

    def greet_peer(k, _):
        greet(peer(k))
        return 0

    lax.fori_loop(1, groups, greet_peer, 0)

    loads = []
    cuts = [(source, sv, 0, deep_s), (source, sv, local - deep_s, deep_s),
            (band, bv, 0, deep_b), (band, bv, local - deep_b, deep_b),
            (source, sv, deep_s, local - 2 * deep_s),
            (band, bv, deep_b, local - 2 * deep_b)]
    for index, (src, dst, at, size) in enumerate(cuts):
        where = pl.ds(at, size)
        loads.append(
            pltpu.make_async_copy(src.at[:, where], dst.at[:, where], local_sem.at[index])
        )
    for load in loads:
        load.start()
    for load in loads[:4]:
        load.wait()
    pl.semaphore_wait(barrier, 2 + GROUP - 1 + groups - 1)
    moves = (
        (sv.at[:, pl.ds(local - deep_s, deep_s)], ls, right),
        (sv.at[:, pl.ds(0, deep_s)], hs, left),
        (bv.at[:, pl.ds(local - deep_b, deep_b)], lb, right),
        (bv.at[:, pl.ds(0, deep_b)], hb, left),
    )
    halo = []
    for index, (src, dst, target) in enumerate(moves):
        halo.append(
            pltpu.make_async_remote_copy(
                src_ref=src, dst_ref=dst, send_sem=hsend.at[index],
                recv_sem=hrecv.at[index], device_id=(target,), device_id_type=MESH,
            )
        )
    for copy in halo:
        copy.start()

    diagonals = band.shape[0]
    places = lax.broadcasted_iota(jnp.int32, (3 * HB, diagonals), 0)
    chosen = jnp.where(places == offsets[...] + HB, 1.0, 0.0).T.astype(BF16)
    chosen = jnp.concatenate([chosen, chosen], axis=0)

    loads[4].wait()

    def turn(at, _):
        z0[block(at + 3)] = pack_columns(sv[:, block(at)])
        return 0

    lax.fori_loop(0, blocks, turn, 0, unroll=4)
    loads[5].wait()

    def build(at, _):
        bands[at + 2] = band_block(bv[:, block(at)], chosen)
        return 0

    lax.fori_loop(0, blocks, build, 0, unroll=4)
    for copy in halo:
        copy.wait()
    for k in range(3):
        part_low = jnp.where(me > 0, ls[:, pl.ds(k * HB, HB)], 0.0)
        part_high = jnp.where(me < n - 1, hs[:, pl.ds(k * HB, HB)], 0.0)
        z0[pl.ds(k * HB, HB)] = pack_columns(part_low)
        z0[pl.ds(3 * HB + local + k * HB, HB)] = pack_columns(part_high)
    for k in range(2):
        part_low = jnp.where(me > 0, lb[:, pl.ds(k * HB, HB)], 0.0)
        part_high = jnp.where(me < n - 1, hb[:, pl.ds(k * HB, HB)], 0.0)
        bands[k] = band_block(part_low, chosen)
        bands[2 + blocks + k] = band_block(part_high, chosen)

    def once(at, _):
        z1[block(at)] = apply_block(bands, z0, at)
        return 0

    lax.fori_loop(0, blocks + 4, once, 0, unroll=4)

    def twice(at, _):
        window = z1[block(at, 3)]
        both = bf(bands[at + 1], jnp.concatenate([window, window], axis=0))
        z2[block(at)] = pack(both + pltpu.roll(both, LANE // 2, 1))
        return 0

    lax.fori_loop(0, blocks + 2, twice, 0, unroll=2)

    def thrice(at, _):
        window = z2[block(at, 3)]
        both = bf(bands[at + 2], jnp.concatenate([window, window], axis=0))
        z3[block(at)] = pack(both + pltpu.roll(both, LANE // 2, 1))
        return 0

    lax.fori_loop(0, blocks, thrice, 0, unroll=4)

    def grow(at, sums):
        first = jnp.concatenate([z0[block(2 * at + 3, 2)], z1[block(2 * at + 2, 2)]], axis=1)
        second = jnp.concatenate([z2[block(2 * at + 1, 2)], z3[block(2 * at, 2)]], axis=1)
        a, b, c = sums
        return (a + bf(first, first, TN), b + bf(first, second, TN), c + bf(second, second, TN))

    zero = jnp.zeros((2 * LANE, 2 * LANE), F32)
    sums = lax.fori_loop(0, blocks // 2, grow, (zero, zero, zero))
    stacked = jnp.concatenate([fold(s) for s in sums], axis=0)
    rows = stacked.shape[0] // GROUP
    mine[...] = stacked.reshape(GROUP, rows, LANE)

    def copy_to(src, dst, send, recv, device):
        return pltpu.make_async_remote_copy(
            src_ref=src, dst_ref=dst, send_sem=send, recv_sem=recv,
            device_id=(device,), device_id_type=MESH,
        )

    ahead = []
    for k in range(1, GROUP):
        to = lax.rem(seat + k, GROUP)
        ahead.append(copy_to(mine.at[to], got.at[k], asend.at[k], arecv.at[k], mate(k)))
    for copy in ahead:
        copy.start()
    summed = mine[seat]
    for k, copy in enumerate(ahead):
        copy.wait_recv()
        summed = summed + got[k + 1]
    part[...] = summed

    def across(k):
        return copy_to(part, gotb.at[k], bsend.at[k], brecv.at[k], peer(k))

    def start(k, _):
        across(k).start()
        return 0

    def arrive(k, value):
        across(k).wait_recv()
        return value + gotb[k]

    lax.fori_loop(1, groups, start, 0)
    summed = lax.fori_loop(1, groups, arrive, summed)
    gathered[seat] = summed
    back = []
    for k in range(1, GROUP):
        back.append(copy_to(gathered.at[seat], gathered.at[seat], csend.at[k], crecv.at[k], mate(k)))
    for copy in back:
        copy.start()
    for copy in back:
        copy.wait_recv()
    gram[...] = gathered[...]
    for copy in ahead + back:
        copy.wait_send()

    def sent(k, _):
        across(k).wait_send()
        return 0

    lax.fori_loop(1, groups, sent, 0)


def make_main(source, band, offsets):
    n = lax.axis_size("rows")
    width, local = source.shape
    diagonals = band.shape[0]
    blocks = local // HB
    groups = n // GROUP
    rows = 3 * LANE // GROUP
    dma = pltpu.SemaphoreType.DMA
    shape = jax.ShapeDtypeStruct
    vm = pltpu.VMEM
    return pl.pallas_call(
        functools.partial(main_kernel, n),
        out_shape=[
            shape((local + 6 * HB, LANE), BF16),
            shape((local + 4 * HB, LANE), BF16),
            shape((local + 2 * HB, LANE), BF16),
            shape((local, LANE), BF16),
            shape((GROUP, rows, LANE), F32),
        ],
        in_specs=[HBM, HBM, VMEM],
        out_specs=[VMEM] * 5,
        scratch_shapes=[
            vm((width, local), F32),
            vm((diagonals, local), F32),
            vm((width, 3 * HB), F32), vm((width, 3 * HB), F32),
            vm((diagonals, 2 * HB), F32), vm((diagonals, 2 * HB), F32),
            vm((blocks + 4, HB, 6 * HB), BF16),
            vm((GROUP, rows, LANE), F32),
            vm((GROUP, rows, LANE), F32),
            vm((rows, LANE), F32),
            vm((groups, rows, LANE), F32),
            vm((GROUP, rows, LANE), F32),
            dma((6,)), dma((4,)), dma((4,)),
            dma((GROUP,)), dma((GROUP,)), dma((groups,)), dma((groups,)),
            dma((GROUP,)), dma((GROUP,)),
        ],
        compiler_params=pltpu.CompilerParams(
            collective_id=0, has_side_effects=True, vmem_limit_bytes=40 << 20
        ),
    )(source, band, offsets.reshape(1, diagonals))


def splat(value):
    return jnp.broadcast_to(value, (SUB, LANE))


def eliminate(metric, right):
    tiles = metric.shape[0] // SUB
    part = [slice(SUB * t, SUB * t + SUB) for t in range(tiles)]
    state = [[metric[part[t]], right[part[t]]] for t in range(tiles)]
    rows = lax.broadcasted_iota(jnp.int32, (SUB, LANE), 0)
    solved = []
    steps = range(SUB)
    for t0 in range(tiles):
        at = SUB * t0
        core = {
            (i, k): splat(state[t0][0][i : i + 1, at + k : at + k + 1])
            for i in steps
            for k in range(i, SUB)
        }
        pivots = [[splat(half[i : i + 1]) for half in state[t0]] for i in steps]
        inverse = []
        for i in steps:
            inverse.append(1.0 / core[i, i])
            for k in range(i + 1, SUB):
                ratio = core[i, k] * inverse[i]
                for m in range(k, SUB):
                    core[k, m] = core[k, m] - ratio * core[i, m]
                pivots[k] = [p - ratio * q for p, q in zip(pivots[k], pivots[i])]
        result = jnp.zeros((SUB, LANE), F32)
        for i in steps:
            result = jnp.where(rows == i, pivots[i][1] * lax.rsqrt(core[i, i]), result)
        solved.append(result)
        for t in range(t0 + 1, tiles):
            scaled = []
            for k in steps:
                column = splat(state[t][0][:, at + k : at + k + 1])
                for i in range(k):
                    column = column - scaled[i] * core[i, k]
                scaled.append(column * inverse[k])
            for half in range(2):
                value = state[t][half]
                for k in steps:
                    value = value - scaled[k] * pivots[k][half]
                state[t][half] = value
    return jnp.concatenate(solved, axis=0)


def compress(grammian, retain):
    spanning = grammian[:retain]
    wide = spanning.shape[1] > retain
    across = lax.broadcasted_iota(jnp.int32, (retain, retain), 1)
    down = lax.broadcasted_iota(jnp.int32, (retain, retain), 0)
    unit = jnp.where(across == down, 1.0, 0.0)
    coeffs = None
    for repeat in range(2):
        if repeat > 0:
            spanning = exact(coeffs, grammian)
        metric = exact(exact(spanning, grammian), spanning, NT)
        metric = 0.5 * (metric + metric.T)
        if wide:
            coeffs = exact(eliminate(metric, unit), spanning)
        else:
            coeffs = eliminate(metric, spanning)
    return coeffs


def last_kernel(total, gram, z0, z1, z2, z3, out, tile, sem):
    keep = LANE
    every = gram[...].reshape(3 * LANE, LANE) * (1.0 / total)
    own, cross, far = every[:keep], every[keep : 2 * keep], every[2 * keep :]
    once = compress(own, keep)
    cross = exact(exact(once, cross), once, NT)
    far = exact(exact(once, far), once, NT)
    across = lax.broadcasted_iota(jnp.int32, (keep, keep), 1)
    down = lax.broadcasted_iota(jnp.int32, (keep, keep), 0)
    unit = jnp.where(across == down, 1.0, 0.0)
    top = jnp.concatenate([unit, cross], axis=1)
    bottom = jnp.concatenate([cross.T, far], axis=1)
    again = compress(jnp.concatenate([top, bottom], axis=0), keep)
    coeffs = jnp.concatenate([exact(again[:, :keep], once), exact(again[:, keep:], once)], axis=1)
    turned = coeffs.T
    half = LANE // 2
    weights = jnp.concatenate(halves(turned), axis=1)
    weights = jnp.concatenate(
        [weights[half * (k // 2) : half * (k // 2) + half] for k in range(8)], axis=0
    )
    local = z3.shape[0]
    count = local // (4 * HB)

    def store(at):
        where = pl.ds(pl.multiple_of(at * 4 * HB, 4 * HB), 4 * HB)
        return pltpu.make_async_copy(tile.at[at], out.at[:, where], sem.at[at])

    def step(at, _):
        where = [pl.ds(pl.multiple_of(at * 4 * HB + k * HB, HB), 4 * HB) for k in (3, 2, 1, 0)]
        lhs = jnp.concatenate([z[w] for z, w in zip((z0, z1, z2, z3), where)], axis=1)
        both = bf(lhs, weights)
        tile[at] = (both[:, :LANE] + both[:, LANE:]).T
        store(at).start()
        return 0

    lax.fori_loop(0, count, step, 0)

    def finish(at, _):
        store(at).wait()
        return 0

    lax.fori_loop(0, count, finish, 0)


def make_last(z0, z1, z2, z3, gram, total):
    local = z3.shape[0]
    count = local // (4 * HB)
    return pl.pallas_call(
        functools.partial(last_kernel, total),
        out_shape=jax.ShapeDtypeStruct((LANE, local), F32),
        in_specs=[VMEM] * 5,
        out_specs=HBM,
        scratch_shapes=[
            pltpu.VMEM((count, LANE, 4 * HB), F32),
            pltpu.SemaphoreType.DMA((count,)),
        ],
        compiler_params=pltpu.CompilerParams(vmem_limit_bytes=28 << 20),
    )(gram, z0, z1, z2, z3)


def body(source, band_values, offsets):
    total = float(source.shape[1] * lax.axis_size("rows"))
    z0, z1, z2, z3, gram = make_main(source, band_values, offsets)
    return make_last(z0, z1, z2, z3, gram, total)


def solution(mesh):
    placed = (P(None, "rows"), P(None, "rows"), P())
    return jax.shard_map(
        body, mesh=mesh, in_specs=placed, out_specs=P(None, "rows"), check_vma=False
    )
```

time: 104 us -> 75.9 us (0.73)
  Pallas kernels: 101 us -> 72 us
    pallas_call x5 -> x1, Pallas kernels: 84.5 us -> 44.4 us  [make_main(): pl.pallas_call(functools.partial(main_kernel, n), out_shape=[shape((local...]
    pallas_call x1, Pallas kernels: 16.1 us -> 27.6 us  [make_last(): pl.pallas_call(functools.partial(last_kernel, total), out_shape=jax.Shape...]
    unnamed x8 -> x6, local copies, waits for them, and re-layouts: 2.82 us -> 3.47 us
where the time goes in v1:
time: 75.9 us; the launch traced here: 75.7 us
  Pallas kernels  72 us (95%)
  local copies, waits for them, and re-layouts  3.47 us (5%)
    pallas_call x1, Pallas kernels, make_main(): pl.pallas_call(functools.partial(main_kernel, n), out_shape=[shape((local...  44.4 us
    pallas_call x1, Pallas kernels, make_last(): pl.pallas_call(functools.partial(last_kernel, total), out_shape=jax.Shape...  27.6 us
    unnamed x6, local copies, waits for them, and re-layouts  3.47 us

profile of v1, /device:TPU:0, one launch (start us, length us, event | category | flops | bytes accessed | tf_op | source)
XLA Modules:
  0.0 75.7 jit_solution(15402489963549405273)
XLA Ops:
  0.0 0.0 copy-start
  0.0 1.6 %copy-done = f32[128,4096]{1,0:T(8,128)S(1)} copy-done((f32[128,4096]{1,0:T(8,128)S(1)}, f32[128,4096]{1,0:T(8,128)}, u32[]{:S(2)}) %copy-start) | copy-done | bytes 2097176
  1.6 0.0 copy-start.1
  1.6 1.2 %copy-done.1 = f32[64,4096]{1,0:T(8,128)S(1)} copy-done((f32[64,4096]{1,0:T(8,128)S(1)}, f32[64,4096]{1,0:T(8,128)}, u32[]{:S(2)}) %copy-start.1) | copy-done | bytes 1048600
  2.8 0.0 copy-start.2
  2.8 0.7 copy-done.2
  3.5 44.4 %shard_map.37 = (bf16[4864,128]{1,0:T(8,128)(2,1)S(1)}, bf16[4608,128]{1,0:T(8,128)(2,1)S(1)}, bf16[4352,128]{1,0:T(8,128)(2,1)S(1)}, bf16[4096,128]{1,0:T(8,128)(2,1)S(1)}, f32[8,48,128]{2,1,0:T(8,128)S(1)}) custom-call(f32[64,4096]{1,0:T(8,128)S(1)} %copy-done.1, f32[128,4096]{1,0:T(8,128)S(1)} %copy-done, s32[1,128]{1,0:T(1,128)S(1)} %bitcast.1), custom_call_target="tpu_custom_call" | custom-call | tf_op jit(solution)/shard_map/pallas_call | solution.py:274
  47.9 27.6 %shard_map.38 = f32[128,4096]{1,0:T(8,128)} custom-call(f32[8,48,128]{2,1,0:T(8,128)S(1)} %get-tuple-element.10.gram, bf16[4864,128]{1,0:T(8,128)(2,1)S(1)} %get-tuple-element.11.z0, bf16[4608,128]{1,0:T(8,128)(2,1)S(1)} %get-tuple-element.12.z1, bf16[4352,128]{1,0:T(8,128)(2,1)S(1)} %get-tuple-element.13.z2, bf16[4096,128]{1,0:T(8,128)(2,1)S(1)} %get-tuple-element.14.z3), custom_call_target="tpu_custom_call" | custom-call | tf_op jit(solution)/shard_map/pallas_call | solution.py:418
Async XLA Ops:
  0.0 1.6 %copy-start = (f32[128,4096]{1,0:T(8,128)S(1)}, f32[128,4096]{1,0:T(8,128)}, u32[]{:S(2)}) copy-start(f32[128,4096]{1,0:T(8,128)} %band.1) | copy-start | bytes 6291460
  1.6 1.2 %copy-start.1 = (f32[64,4096]{1,0:T(8,128)S(1)}, f32[64,4096]{1,0:T(8,128)}, u32[]{:S(2)}) copy-start(f32[64,4096]{1,0:T(8,128)} %source.1) | copy-start | bytes 3145732
  2.8 0.7 copy-start.2

commit v2 on v1

v2 whole, which is shorter than its diff:
```python
import functools

import jax
import jax.numpy as jnp
from jax import lax
from jax.experimental import pallas as pl
from jax.experimental.pallas import tpu as pltpu
from jax.sharding import PartitionSpec as P

HB = 128
SUB = 8
LANE = 128
GROUP = 8
MESH = pl.DeviceIdType.MESH
VMEM = pl.BlockSpec(memory_space=pltpu.VMEM)
HBM = pl.BlockSpec(memory_space=pltpu.HBM)
NN = (((1,), (0,)), ((), ()))
NT = (((1,), (1,)), ((), ()))
TN = (((0,), (0,)), ((), ()))
F32 = jnp.float32
BF16 = jnp.bfloat16


def exact(a, b, dims=NN):
    return lax.dot_general(
        a, b, dims, precision=lax.Precision.HIGHEST, preferred_element_type=F32
    )


def bf(a, b, dims=NN):
    return lax.dot_general(a, b, dims, preferred_element_type=F32)


def halves(value):
    high = value.astype(BF16)
    low = (value - high.astype(F32)).astype(BF16)
    return high, low


def block(at, count=1):
    return pl.ds(pl.multiple_of(at * HB, HB), count * HB)


def pack(twice, flip):
    lanes = lax.broadcasted_iota(jnp.int32, twice.shape, 1)
    high = twice.astype(BF16).astype(F32)
    return jnp.where((lanes < LANE // 2) != flip, high, twice - high).astype(BF16)


def pack_columns(part):
    return pack(jnp.concatenate([part, part], axis=0).T, False)


def band_block(values, chosen):
    top, bottom = halves(values.T)
    spread = bf(jnp.concatenate([top, bottom], axis=1), chosen)
    sheared = pltpu.roll(spread, 0, 1, stride=1, stride_axis=0)
    return jnp.concatenate(halves(sheared), axis=1)


def apply_band(bands, skip, z, out, flip):
    def step(at, _):
        window = z[block(at, 3)]
        both = bf(bands[at + skip], jnp.concatenate([window, window], axis=0))
        out[block(at)] = pack(both + pltpu.roll(both, LANE // 2, 1), flip)
        return 0

    blocks = out.shape[0] // HB
    lax.fori_loop(0, blocks, step, 0, unroll=blocks)


def swap(value):
    return pltpu.roll(value, LANE // 2, 1)


def mixed(even, odd):
    lanes = lax.broadcasted_iota(jnp.int32, even.shape, 1)
    first = lanes < LANE // 2
    return jnp.where(first, even, odd), jnp.where(first, odd, even)


class Total:
    def __init__(self, n, refs):
        self.groups = n // GROUP
        me = lax.axis_index("rows")
        self.team, self.seat = me // GROUP, lax.rem(me, GROUP)
        (self.mine, self.got, self.part, self.gotb, self.gathered,
         self.asend, self.arecv, self.bsend, self.brecv, self.csend, self.crecv) = refs

    def mate(self, k):
        return self.team * GROUP + lax.rem(self.seat + k, GROUP)

    def peer(self, k):
        return lax.rem(self.team + k, self.groups) * GROUP + self.seat

    def copy(self, src, dst, send, recv, device):
        return pltpu.make_async_remote_copy(
            src_ref=src, dst_ref=dst, send_sem=send, recv_sem=recv,
            device_id=(device,), device_id_type=MESH,
        )

    def ahead(self, k):
        to = lax.rem(self.seat + k, GROUP)
        return self.copy(
            self.mine.at[to], self.got.at[k], self.asend.at[k], self.arecv.at[k], self.mate(k)
        )

    def across(self, k):
        return self.copy(
            self.part, self.gotb.at[k], self.bsend.at[k], self.brecv.at[k], self.peer(k)
        )

    def back(self, k):
        own = self.gathered.at[self.seat]
        return self.copy(own, own, self.csend.at[k], self.crecv.at[k], self.mate(k))

    def scatter(self, value):
        self.mine[...] = value.reshape(self.mine.shape)
        for k in range(1, GROUP):
            self.ahead(k).start()

    def middle(self):
        summed = self.mine[self.seat]
        for k in range(1, GROUP):
            self.ahead(k).wait_recv()
            summed = summed + self.got[k]
        self.part[...] = summed

        def start(k, _):
            self.across(k).start()
            return 0

        lax.fori_loop(1, self.groups, start, 0)

    def post(self):
        def arrive(k, value):
            self.across(k).wait_recv()
            return value + self.gotb[k]

        self.gathered[self.seat] = lax.fori_loop(1, self.groups, arrive, self.part[...])
        for k in range(1, GROUP):
            self.back(k).start()

    def finish(self):
        for k in range(1, GROUP):
            self.back(k).wait_recv()
        value = self.gathered[...].reshape(GROUP * self.part.shape[0], LANE)
        for k in range(1, GROUP):
            self.ahead(k).wait_send()
            self.back(k).wait_send()

        def sent(k, _):
            self.across(k).wait_send()
            return 0

        lax.fori_loop(1, self.groups, sent, 0)
        return value

    @staticmethod
    def scratch(n, rows):
        groups, share = n // GROUP, rows // GROUP
        vm, dma = pltpu.VMEM, pltpu.SemaphoreType.DMA
        return [
            vm((GROUP, share, LANE), F32), vm((GROUP, share, LANE), F32),
            vm((share, LANE), F32), vm((groups, share, LANE), F32),
            vm((GROUP, share, LANE), F32),
            dma((GROUP,)), dma((GROUP,)), dma((groups,)), dma((groups,)),
            dma((GROUP,)), dma((GROUP,)),
        ]


def main_kernel(
    n, total, source, band, offsets,
    z0, z1, z2, z3, once, gram,
    sv, bv, ov, ls, hs, lb, hb, bands, local_sem, hsend, hrecv, *totals
):
    me = lax.axis_index("rows")
    right, left = lax.rem(me + 1, n), lax.rem(me + n - 1, n)
    near = Total(n, totals[: len(totals) // 2])
    far = Total(n, totals[len(totals) // 2 :])
    local = source.shape[1]
    blocks = local // HB
    deep_s, deep_b = 3 * HB, 2 * HB
    barrier = pltpu.get_barrier_semaphore()

    def greet(device):
        pl.semaphore_signal(barrier, inc=1, device_id=(device,), device_id_type=MESH)

    def greet_peer(k, _):
        greet(near.peer(k))
        return 0

    greet(left)
    greet(right)
    lax.fori_loop(1, near.groups, greet_peer, 0)
    for k in range(1, GROUP):
        greet(near.mate(k))
    whole = pl.ds(0, offsets.shape[1])
    cuts = [
        (source, sv, pl.ds(0, deep_s)), (source, sv, pl.ds(local - deep_s, deep_s)),
        (band, bv, pl.ds(0, deep_b)), (band, bv, pl.ds(local - deep_b, deep_b)),
        (offsets, ov, whole),
        (source, sv, pl.ds(deep_s, local - 2 * deep_s)),
        (band, bv, pl.ds(deep_b, local - 2 * deep_b)),
    ]
    loads = [
        pltpu.make_async_copy(src.at[:, where], dst.at[:, where], local_sem.at[index])
        for index, (src, dst, where) in enumerate(cuts)
    ]
    for load in loads:
        load.start()
    for load in loads[:4]:
        load.wait()
    pl.semaphore_wait(barrier, 2 + GROUP - 1 + near.groups - 1)
    moves = (
        (sv.at[:, pl.ds(local - deep_s, deep_s)], ls, right),
        (sv.at[:, pl.ds(0, deep_s)], hs, left),
        (bv.at[:, pl.ds(local - deep_b, deep_b)], lb, right),
        (bv.at[:, pl.ds(0, deep_b)], hb, left),
    )
    halo = [
        near.copy(src, dst, hsend.at[index], hrecv.at[index], target)
        for index, (src, dst, target) in enumerate(moves)
    ]
    for copy in halo:
        copy.start()

    loads[4].wait()
    diagonals = band.shape[0]
    places = lax.broadcasted_iota(jnp.int32, (3 * HB, diagonals), 0)
    chosen = jnp.where(places == ov[...] + HB, 1.0, 0.0).T.astype(BF16)
    chosen = jnp.concatenate([chosen, chosen], axis=0)
    loads[5].wait()

    def turn(at, _):
        z0[block(at + 3)] = pack_columns(sv[:, block(at)])
        return 0

    lax.fori_loop(0, blocks, turn, 0, unroll=blocks // 2)
    loads[6].wait()

    def build(at, _):
        bands[at + 2] = band_block(bv[:, block(at)], chosen)
        return 0

    lax.fori_loop(0, blocks, build, 0, unroll=blocks)
    for copy in halo:
        copy.wait_recv()
    for k in range(3):
        part_low = jnp.where(me > 0, ls[:, pl.ds(k * HB, HB)], 0.0)
        part_high = jnp.where(me < n - 1, hs[:, pl.ds(k * HB, HB)], 0.0)
        z0[pl.ds(k * HB, HB)] = pack_columns(part_low)
        z0[pl.ds(3 * HB + local + k * HB, HB)] = pack_columns(part_high)
    for k in range(2):
        part_low = jnp.where(me > 0, lb[:, pl.ds(k * HB, HB)], 0.0)
        part_high = jnp.where(me < n - 1, hb[:, pl.ds(k * HB, HB)], 0.0)
        bands[k] = band_block(part_low, chosen)
        bands[2 + blocks + k] = band_block(part_high, chosen)
    apply_band(bands, 0, z0, z1, True)
    inner0, inner1 = z0[pl.ds(3 * HB, local)], z1[pl.ds(2 * HB, local)]
    high, low = mixed(inner0, inner1)
    product = bf(high, jnp.concatenate([high, low], axis=1), TN)
    cross = swap(product[:, LANE:])
    near.scatter(product[:, :LANE] + cross + cross.T)

    apply_band(bands, 1, z1, z2, False)
    apply_band(bands, 2, z2, z3, True)
    near.middle()
    high, low = mixed(z0[pl.ds(3 * HB, local)], z1[pl.ds(2 * HB, local)])
    high2, low2 = mixed(z2[pl.ds(HB, local)], z3[...])
    product = bf(high2, jnp.concatenate([high, low, high2, low2], axis=1), TN)
    other = bf(high, low2, TN)
    cross = (product[:, :LANE] + swap(product[:, LANE : 2 * LANE])).T + swap(other)
    own = swap(product[:, 3 * LANE :])
    own = product[:, 2 * LANE : 3 * LANE] + own + own.T
    far.scatter(jnp.concatenate([cross, own], axis=0))
    near.post()
    far.middle()
    gram_one = near.finish() * (1.0 / total)
    turned = square_turn(gram_one, gram_one)
    far.post()
    once[...] = square_turn(exact(turned, gram_one), gram_one)
    gram[...] = far.finish() * (1.0 / total)
    for copy in halo:
        copy.wait_send()


def make_main(source, band, offsets, total):
    n = lax.axis_size("rows")
    width, local = source.shape
    diagonals = band.shape[0]
    blocks = local // HB
    dma = pltpu.SemaphoreType.DMA
    shape = jax.ShapeDtypeStruct
    vm = pltpu.VMEM
    return pl.pallas_call(
        functools.partial(main_kernel, n, total),
        out_shape=[
            shape((local + 6 * HB, LANE), BF16),
            shape((local + 4 * HB, LANE), BF16),
            shape((local + 2 * HB, LANE), BF16),
            shape((local, LANE), BF16),
            shape((LANE, LANE), F32),
            shape((2 * LANE, LANE), F32),
        ],
        in_specs=[HBM] * 3,
        out_specs=[VMEM] * 6,
        scratch_shapes=[
            vm((width, local), F32),
            vm((diagonals, local), F32),
            vm((1, diagonals), jnp.int32),
            vm((width, 3 * HB), F32), vm((width, 3 * HB), F32),
            vm((diagonals, 2 * HB), F32), vm((diagonals, 2 * HB), F32),
            vm((blocks + 4, HB, 6 * HB), BF16),
            dma((7,)), dma((4,)), dma((4,)),
        ]
        + Total.scratch(n, LANE)
        + Total.scratch(n, 2 * LANE),
        compiler_params=pltpu.CompilerParams(
            collective_id=0, has_side_effects=True, vmem_limit_bytes=46 << 20
        ),
    )(source, band, offsets.reshape(1, diagonals))


def splat(value):
    return jnp.broadcast_to(value, (SUB, LANE))


def eliminate(metric, right):
    tiles = metric.shape[0] // SUB
    part = [slice(SUB * t, SUB * t + SUB) for t in range(tiles)]
    state = [[metric[part[t]], right[part[t]]] for t in range(tiles)]
    rows = lax.broadcasted_iota(jnp.int32, (SUB, LANE), 0)
    solved = []
    steps = range(SUB)
    for t0 in range(tiles):
        at = SUB * t0
        core = {
            (i, k): splat(state[t0][0][i : i + 1, at + k : at + k + 1])
            for i in steps
            for k in range(i, SUB)
        }
        pivots = [[splat(half[i : i + 1]) for half in state[t0]] for i in steps]
        inverse = []
        for i in steps:
            inverse.append(1.0 / core[i, i])
            for k in range(i + 1, SUB):
                ratio = core[i, k] * inverse[i]
                for m in range(k, SUB):
                    core[k, m] = core[k, m] - ratio * core[i, m]
                pivots[k] = [p - ratio * q for p, q in zip(pivots[k], pivots[i])]
        result = jnp.zeros((SUB, LANE), F32)
        for i in steps:
            result = jnp.where(rows == i, pivots[i][1] * lax.rsqrt(core[i, i]), result)
        solved.append(result)
        for t in range(t0 + 1, tiles):
            scaled = []
            for k in steps:
                column = splat(state[t][0][:, at + k : at + k + 1])
                for i in range(k):
                    column = column - scaled[i] * core[i, k]
                scaled.append(column * inverse[k])
            for half in range(2):
                value = state[t][half]
                for k in steps:
                    value = value - scaled[k] * pivots[k][half]
                state[t][half] = value
    return jnp.concatenate(solved, axis=0)


def square_turn(spanning, grammian):
    return eliminate(exact(exact(spanning, grammian), spanning, NT), spanning)


def last_kernel(once, gram, z0, z1, z2, z3, out, tile, sem):
    keep = LANE
    coeffs = once[...]
    cross, far = gram[:keep], gram[keep:]
    cross = exact(exact(coeffs, cross), coeffs, NT)
    far = exact(exact(coeffs, far), coeffs, NT)
    across = lax.broadcasted_iota(jnp.int32, (keep, keep), 1)
    down = lax.broadcasted_iota(jnp.int32, (keep, keep), 0)
    unit = jnp.where(across == down, 1.0, 0.0)
    span_a = unit + exact(cross, cross, NT)
    span_b = cross + exact(cross, far)
    next_a = span_a + exact(span_b, cross, NT)
    next_b = exact(span_a, cross) + exact(span_b, far)
    metric = exact(next_a, span_a, NT) + exact(next_b, span_b, NT)
    spanning = jnp.concatenate([exact(span_a, coeffs), exact(span_b, coeffs)], axis=1)
    coeffs = exact(eliminate(metric, unit), spanning)
    turned = coeffs.T
    half = LANE // 2
    weights = jnp.concatenate(halves(turned), axis=1)
    weights = jnp.concatenate(
        [weights[half * (k // 2) : half * (k // 2) + half] for k in range(8)], axis=0
    )
    local = z3.shape[0]
    count = local // (4 * HB)

    def store(at):
        where = pl.ds(pl.multiple_of(at * 4 * HB, 4 * HB), 4 * HB)
        return pltpu.make_async_copy(tile.at[at], out.at[:, where], sem.at[at])

    def step(at, _):
        where = [pl.ds(pl.multiple_of(at * 4 * HB + k * HB, HB), 4 * HB) for k in (3, 2, 1, 0)]
        lhs = jnp.concatenate([z[w] for z, w in zip((z0, z1, z2, z3), where)], axis=1)
        both = bf(lhs, weights)
        tile[at] = (both[:, :LANE] + both[:, LANE:]).T
        store(at).start()
        return 0

    lax.fori_loop(0, count, step, 0, unroll=count)

    def finish(at, _):
        store(at).wait()
        return 0

    lax.fori_loop(0, count, finish, 0)


def make_last(once, gram, z0, z1, z2, z3):
    local = z3.shape[0]
    count = local // (4 * HB)
    return pl.pallas_call(
        last_kernel,
        out_shape=jax.ShapeDtypeStruct((LANE, local), F32),
        in_specs=[VMEM] * 6,
        out_specs=HBM,
        scratch_shapes=[
            pltpu.VMEM((count, LANE, 4 * HB), F32),
            pltpu.SemaphoreType.DMA((count,)),
        ],
        compiler_params=pltpu.CompilerParams(vmem_limit_bytes=28 << 20),
    )(once, gram, z0, z1, z2, z3)


def body(source, band_values, offsets):
    total = float(source.shape[1] * lax.axis_size("rows"))
    z0, z1, z2, z3, once, gram = make_main(source, band_values, offsets, total)
    return make_last(once, gram, z0, z1, z2, z3)


def solution(mesh):
    placed = (P(None, "rows"), P(None, "rows"), P())
    return jax.shard_map(
        body, mesh=mesh, in_specs=placed, out_specs=P(None, "rows"), check_vma=False
    )
```

time: 75.9 us -> 49.7 us (0.65)
  Pallas kernels: 72 us -> 45.9 us
    pallas_call x2, Pallas kernels: 72 us -> 45.9 us  [the longest x1 36.8 us: make_main(): pl.pallas_call(functools.partial(main_kernel, n, total), out_shape=[shape...]
where the time goes in v2:
time: 49.7 us; the launch traced here: 49.5 us
  Pallas kernels  45.9 us (92%)
  local copies, waits for them, and re-layouts  3.47 us (7%)
    pallas_call x1, Pallas kernels, make_main(): pl.pallas_call(functools.partial(main_kernel, n, total), out_shape=[shape...  36.8 us
    pallas_call x1, Pallas kernels, make_last(): pl.pallas_call(last_kernel, out_shape=jax.ShapeDtypeStruct((LANE, local),...  9.13 us
    unnamed x6, local copies, waits for them, and re-layouts  3.47 us

profile of v2, /device:TPU:0, one launch (start us, length us, event | category | flops | bytes accessed | tf_op | source)
XLA Modules:
  0.0 49.5 jit_solution(1503705943198142417)
XLA Ops:
  0.0 0.0 copy-start
  0.0 1.6 %copy-done = f32[128,4096]{1,0:T(8,128)S(1)} copy-done((f32[128,4096]{1,0:T(8,128)S(1)}, f32[128,4096]{1,0:T(8,128)}, u32[]{:S(2)}) %copy-start) | copy-done | bytes 2097176
  1.6 0.0 copy-start.1
  1.6 1.2 %copy-done.1 = f32[64,4096]{1,0:T(8,128)S(1)} copy-done((f32[64,4096]{1,0:T(8,128)S(1)}, f32[64,4096]{1,0:T(8,128)}, u32[]{:S(2)}) %copy-start.1) | copy-done | bytes 1048600
  2.8 0.0 copy-start.2
  2.8 0.7 %copy-done.2 = s32[128]{0:T(128)S(1)} copy-done((s32[128]{0:T(128)S(1)}, s32[128]{0:T(128)}, u32[]{:S(2)}) %copy-start.2) | copy-done | bytes 536
  3.5 36.8 %shard_map.37 = (bf16[4864,128]{1,0:T(8,128)(2,1)S(1)}, bf16[4608,128]{1,0:T(8,128)(2,1)S(1)}, bf16[4352,128]{1,0:T(8,128)(2,1)S(1)}, bf16[4096,128]{1,0:T(8,128...) custom-call(f32[64,4096]{1,0:T(8,128)S(1)} %copy-done.1, f32[128,4096]{1,0:T(8,128)S(1)} %copy-done, ...), custom_call_target="tpu_custom_call" | custom-call | tf_op jit(solution)/shard_map/pallas_call | solution.py:296
  40.2 9.1 %shard_map.38 = f32[128,4096]{1,0:T(8,128)} custom-call(f32[128,128]{1,0:T(8,128)S(1)} %get-tuple-element.11.once, f32[256,128]{1,0:T(8,128)S(1)} %get-tuple-element.12.gram, bf16[4864,128]{1,0:T(8,128)(2,1)S(1)} %get-tuple-element.13.z0, bf16[4608,128]{1,0:T(8,128)(2,1)S(1)} %get-tuple-element.14.z1, bf16[4352,128]{1,0:T(8,128)(2,1)S(1)} %get-tuple-element.15.z2, ...), custom_call_target="tpu_custom_call" | custom-call | tf_op jit(solution)/shard_map/pallas_call | solution.py:424
Async XLA Ops:
  0.0 1.6 %copy-start = (f32[128,4096]{1,0:T(8,128)S(1)}, f32[128,4096]{1,0:T(8,128)}, u32[]{:S(2)}) copy-start(f32[128,4096]{1,0:T(8,128)} %band.1) | copy-start | bytes 6291460
  1.6 1.2 %copy-start.1 = (f32[64,4096]{1,0:T(8,128)S(1)}, f32[64,4096]{1,0:T(8,128)}, u32[]{:S(2)}) copy-start(f32[64,4096]{1,0:T(8,128)} %source.1) | copy-start | bytes 3145732
  2.8 0.7 %copy-start.2 = (s32[128]{0:T(128)S(1)}, s32[128]{0:T(128)}, u32[]{:S(2)}) copy-start(s32[128]{0:T(128)} %param.5) | copy-start | bytes 1540

commit v3 on v2

--- a/solution.py
+++ b/solution.py
@@ -11,6 +11,7 @@
 SUB = 8
 LANE = 128
 GROUP = 8
+PIECE = 4 * HB
 MESH = pl.DeviceIdType.MESH
 VMEM = pl.BlockSpec(memory_space=pltpu.VMEM)
 HBM = pl.BlockSpec(memory_space=pltpu.HBM)
@@ -58,15 +59,15 @@
     return jnp.concatenate(halves(sheared), axis=1)
 
 
-def apply_band(bands, skip, z, out, flip):
-    def step(at, _):
+def apply_band(bands, skip, z, out, flip, start, count):
+    def step(k, _):
+        at = start + k
         window = z[block(at, 3)]
         both = bf(bands[at + skip], jnp.concatenate([window, window], axis=0))
         out[block(at)] = pack(both + pltpu.roll(both, LANE // 2, 1), flip)
         return 0
 
-    blocks = out.shape[0] // HB
-    lax.fori_loop(0, blocks, step, 0, unroll=blocks)
+    lax.fori_loop(0, count, step, 0, unroll=count)
 
 
 def swap(value):
@@ -170,10 +171,12 @@
 
 
 def main_kernel(
-    n, total, source, band, offsets,
-    z0, z1, z2, z3, once, gram,
-    sv, bv, ov, ls, hs, lb, hb, bands, local_sem, hsend, hrecv, *totals
+    n, total, source, band, offsets, *rest
 ):
+    pieces = source.shape[1] // PIECE
+    packs, (once, gram) = rest[:pieces], rest[pieces : pieces + 2]
+    (z0, z1, z2, z3, sv, bv, ov, ls, hs, lb, hb, bands,
+     local_sem, hsend, hrecv, *totals) = rest[pieces + 2 :]
     me = lax.axis_index("rows")
     right, left = lax.rem(me + 1, n), lax.rem(me + n - 1, n)
     near = Total(n, totals[: len(totals) // 2])
@@ -196,12 +199,12 @@
     for k in range(1, GROUP):
         greet(near.mate(k))
     whole = pl.ds(0, offsets.shape[1])
+    half = local // 2
     cuts = [
         (source, sv, pl.ds(0, deep_s)), (source, sv, pl.ds(local - deep_s, deep_s)),
-        (band, bv, pl.ds(0, deep_b)), (band, bv, pl.ds(local - deep_b, deep_b)),
+        (source, sv, pl.ds(deep_s, local - 2 * deep_s)),
         (offsets, ov, whole),
-        (source, sv, pl.ds(deep_s, local - 2 * deep_s)),
-        (band, bv, pl.ds(deep_b, local - 2 * deep_b)),
+        (band, bv, pl.ds(0, half)), (band, bv, pl.ds(half, half)),
     ]
     loads = [
         pltpu.make_async_copy(src.at[:, where], dst.at[:, where], local_sem.at[index])
@@ -211,12 +214,36 @@
         load.start()
     for load in loads[:4]:
         load.wait()
+    diagonals = band.shape[0]
+    places = lax.broadcasted_iota(jnp.int32, (3 * HB, diagonals), 0)
+    chosen = jnp.where(places == ov[...] + HB, 1.0, 0.0).T.astype(BF16)
+    chosen = jnp.concatenate([chosen, chosen], axis=0)
+
+    def turn(at, _):
+        z0[block(at + 3)] = pack_columns(sv[:, block(at)])
+        return 0
+
+    lax.fori_loop(0, blocks, turn, 0, unroll=blocks // 2)
+
+    def build(at, _):
+        bands[at + 2] = band_block(bv[:, block(at)], chosen)
+        return 0
+
+    loads[4].wait()
+    lax.fori_loop(0, blocks // 2, build, 0, unroll=blocks // 2)
+    loads[5].wait()
     pl.semaphore_wait(barrier, 2 + GROUP - 1 + near.groups - 1)
+    near_low, near_high = pl.ds(0, HB), pl.ds(local - HB, HB)
+    far_low, far_high = pl.ds(HB, deep_b), pl.ds(local - deep_s, deep_b)
+    own_low, own_high = pl.ds(0, deep_b), pl.ds(local - deep_b, deep_b)
+    last, first = pl.ds(deep_b, HB), pl.ds(0, HB)
     moves = (
-        (sv.at[:, pl.ds(local - deep_s, deep_s)], ls, right),
-        (sv.at[:, pl.ds(0, deep_s)], hs, left),
-        (bv.at[:, pl.ds(local - deep_b, deep_b)], lb, right),
-        (bv.at[:, pl.ds(0, deep_b)], hb, left),
+        (sv.at[:, near_high], ls.at[:, last], right),
+        (sv.at[:, near_low], hs.at[:, first], left),
+        (sv.at[:, far_high], ls.at[:, own_low], right),
+        (sv.at[:, far_low], hs.at[:, far_low], left),
+        (bv.at[:, own_high], lb, right),
+        (bv.at[:, own_low], hb, left),
     )
     halo = [
         near.copy(src, dst, hsend.at[index], hrecv.at[index], target)
@@ -224,48 +251,39 @@
     ]
     for copy in halo:
         copy.start()
-
-    loads[4].wait()
-    diagonals = band.shape[0]
-    places = lax.broadcasted_iota(jnp.int32, (3 * HB, diagonals), 0)
-    chosen = jnp.where(places == ov[...] + HB, 1.0, 0.0).T.astype(BF16)
-    chosen = jnp.concatenate([chosen, chosen], axis=0)
-    loads[5].wait()
-
-    def turn(at, _):
-        z0[block(at + 3)] = pack_columns(sv[:, block(at)])
-        return 0
-
-    lax.fori_loop(0, blocks, turn, 0, unroll=blocks // 2)
-    loads[6].wait()
-
-    def build(at, _):
-        bands[at + 2] = band_block(bv[:, block(at)], chosen)
-        return 0
-
-    lax.fori_loop(0, blocks, build, 0, unroll=blocks)
-    for copy in halo:
+    lax.fori_loop(blocks // 2, blocks, build, 0, unroll=blocks // 2)
+    apply_band(bands, 0, z0, z1, True, 3, blocks - 2)
+
+    def edge_source(k):
+        part_low = jnp.where(me > 0, ls[:, pl.ds(k * HB, HB)], 0.0)
+        z0[pl.ds(k * HB, HB)] = pack_columns(part_low)
+        k = 2 - k
+        part_high = jnp.where(me < n - 1, hs[:, pl.ds(k * HB, HB)], 0.0)
+        z0[pl.ds(3 * HB + local + k * HB, HB)] = pack_columns(part_high)
+
+    for copy in halo[:2]:
         copy.wait_recv()
-    for k in range(3):
-        part_low = jnp.where(me > 0, ls[:, pl.ds(k * HB, HB)], 0.0)
-        part_high = jnp.where(me < n - 1, hs[:, pl.ds(k * HB, HB)], 0.0)
-        z0[pl.ds(k * HB, HB)] = pack_columns(part_low)
-        z0[pl.ds(3 * HB + local + k * HB, HB)] = pack_columns(part_high)
+    edge_source(2)
+    apply_band(bands, 0, z0, z1, True, 2, 1)
+    apply_band(bands, 0, z0, z1, True, blocks + 1, 1)
+    high, low = mixed(z0[pl.ds(3 * HB, local)], z1[pl.ds(2 * HB, local)])
+    product = bf(high, jnp.concatenate([high, low], axis=1), TN)
+    cross = swap(product[:, LANE:])
+    near.scatter(product[:, :LANE] + cross + cross.T)
+
+    for copy in halo[2:]:
+        copy.wait_recv()
     for k in range(2):
+        edge_source(k)
         part_low = jnp.where(me > 0, lb[:, pl.ds(k * HB, HB)], 0.0)
         part_high = jnp.where(me < n - 1, hb[:, pl.ds(k * HB, HB)], 0.0)
         bands[k] = band_block(part_low, chosen)
         bands[2 + blocks + k] = band_block(part_high, chosen)
-    apply_band(bands, 0, z0, z1, True)
-    inner0, inner1 = z0[pl.ds(3 * HB, local)], z1[pl.ds(2 * HB, local)]
-    high, low = mixed(inner0, inner1)
-    product = bf(high, jnp.concatenate([high, low], axis=1), TN)
-    cross = swap(product[:, LANE:])
-    near.scatter(product[:, :LANE] + cross + cross.T)
-
-    apply_band(bands, 1, z1, z2, False)
-    apply_band(bands, 2, z2, z3, True)
+    apply_band(bands, 0, z0, z1, True, 0, 2)
+    apply_band(bands, 0, z0, z1, True, blocks + 2, 2)
+    apply_band(bands, 1, z1, z2, False, 0, blocks + 2)
     near.middle()
+    apply_band(bands, 2, z2, z3, True, 0, blocks)
     high, low = mixed(z0[pl.ds(3 * HB, local)], z1[pl.ds(2 * HB, local)])
     high2, low2 = mixed(z2[pl.ds(HB, local)], z3[...])
     product = bf(high2, jnp.concatenate([high, low, high2, low2], axis=1), TN)
@@ -274,6 +292,10 @@
     own = swap(product[:, 3 * LANE :])
     own = product[:, 2 * LANE : 3 * LANE] + own + own.T
     far.scatter(jnp.concatenate([cross, own], axis=0))
+    for index, out in enumerate(packs):
+        for at, z in enumerate((z0, z1, z2, z3)):
+            where = pl.ds(index * PIECE + (3 - at) * HB, PIECE)
+            out[:, at * LANE : (at + 1) * LANE] = z[where]
     near.post()
     far.middle()
     gram_one = near.finish() * (1.0 / total)
@@ -296,28 +318,28 @@
     return pl.pallas_call(
         functools.partial(main_kernel, n, total),
         out_shape=[
-            shape((local + 6 * HB, LANE), BF16),
-            shape((local + 4 * HB, LANE), BF16),
-            shape((local + 2 * HB, LANE), BF16),
-            shape((local, LANE), BF16),
-            shape((LANE, LANE), F32),
-            shape((2 * LANE, LANE), F32),
-        ],
+            shape((PIECE, 4 * LANE), BF16) for _ in range(local // PIECE)
+        ]
+        + [shape((LANE, LANE), F32), shape((2 * LANE, LANE), F32)],
         in_specs=[HBM] * 3,
-        out_specs=[VMEM] * 6,
+        out_specs=[VMEM] * (local // PIECE + 2),
         scratch_shapes=[
+            vm((local + 6 * HB, LANE), BF16),
+            vm((local + 4 * HB, LANE), BF16),
+            vm((local + 2 * HB, LANE), BF16),
+            vm((local, LANE), BF16),
             vm((width, local), F32),
             vm((diagonals, local), F32),
             vm((1, diagonals), jnp.int32),
             vm((width, 3 * HB), F32), vm((width, 3 * HB), F32),
             vm((diagonals, 2 * HB), F32), vm((diagonals, 2 * HB), F32),
             vm((blocks + 4, HB, 6 * HB), BF16),
-            dma((7,)), dma((4,)), dma((4,)),
+            dma((6,)), dma((6,)), dma((6,)),
         ]
         + Total.scratch(n, LANE)
         + Total.scratch(n, 2 * LANE),
         compiler_params=pltpu.CompilerParams(
-            collective_id=0, has_side_effects=True, vmem_limit_bytes=46 << 20
+            collective_id=0, has_side_effects=True, vmem_limit_bytes=49 << 20
         ),
     )(source, band, offsets.reshape(1, diagonals))
 
@@ -372,7 +394,8 @@
     return eliminate(exact(exact(spanning, grammian), spanning, NT), spanning)
 
 
-def last_kernel(once, gram, z0, z1, z2, z3, out, tile, sem):
+def last_kernel(once, gram, *rest):
+    *packs, out, tile, sem = rest
     keep = LANE
     coeffs = once[...]
     cross, far = gram[:keep], gram[keep:]
@@ -394,50 +417,39 @@
     weights = jnp.concatenate(
         [weights[half * (k // 2) : half * (k // 2) + half] for k in range(8)], axis=0
     )
-    local = z3.shape[0]
-    count = local // (4 * HB)
-
-    def store(at):
-        where = pl.ds(pl.multiple_of(at * 4 * HB, 4 * HB), 4 * HB)
-        return pltpu.make_async_copy(tile.at[at], out.at[:, where], sem.at[at])
-
-    def step(at, _):
-        where = [pl.ds(pl.multiple_of(at * 4 * HB + k * HB, HB), 4 * HB) for k in (3, 2, 1, 0)]
-        lhs = jnp.concatenate([z[w] for z, w in zip((z0, z1, z2, z3), where)], axis=1)
-        both = bf(lhs, weights)
+    stores = []
+    for at, piece in enumerate(packs):
+        both = bf(piece[...], weights)
         tile[at] = (both[:, :LANE] + both[:, LANE:]).T
-        store(at).start()
-        return 0
-
-    lax.fori_loop(0, count, step, 0, unroll=count)
-
-    def finish(at, _):
-        store(at).wait()
-        return 0
-
-    lax.fori_loop(0, count, finish, 0)
-
-
-def make_last(once, gram, z0, z1, z2, z3):
-    local = z3.shape[0]
-    count = local // (4 * HB)
+        stores.append(
+            pltpu.make_async_copy(
+                tile.at[at], out.at[:, pl.ds(at * PIECE, PIECE)], sem.at[at]
+            )
+        )
+        stores[-1].start()
+    for store in stores:
+        store.wait()
+
+
+def make_last(packs, once, gram):
+    count = len(packs)
     return pl.pallas_call(
         last_kernel,
-        out_shape=jax.ShapeDtypeStruct((LANE, local), F32),
-        in_specs=[VMEM] * 6,
+        out_shape=jax.ShapeDtypeStruct((LANE, count * PIECE), F32),
+        in_specs=[VMEM] * (count + 2),
         out_specs=HBM,
         scratch_shapes=[
-            pltpu.VMEM((count, LANE, 4 * HB), F32),
+            pltpu.VMEM((count, LANE, PIECE), F32),
             pltpu.SemaphoreType.DMA((count,)),
         ],
         compiler_params=pltpu.CompilerParams(vmem_limit_bytes=28 << 20),
-    )(once, gram, z0, z1, z2, z3)
+    )(once, gram, *packs)
 
 
 def body(source, band_values, offsets):
     total = float(source.shape[1] * lax.axis_size("rows"))
-    z0, z1, z2, z3, once, gram = make_main(source, band_values, offsets, total)
-    return make_last(once, gram, z0, z1, z2, z3)
+    *packs, once, gram = make_main(source, band_values, offsets, total)
+    return make_last(packs, once, gram)
 
 
 def solution(mesh):

time: 49.7 us -> 44.2 us (0.89)
  local copies, waits for them, and re-layouts: 3.47 us -> 0.65 us
  Pallas kernels: 45.9 us -> 43.2 us
    unnamed x6 -> x2, local copies, waits for them, and re-layouts: 3.47 us -> 0.65 us
    pallas_call x1, Pallas kernels: 36.8 us -> 34.1 us  [make_main(): pl.pallas_call(functools.partial(main_kernel, n, total), out_shape=[shape...]
where the time goes in v3:
time: 44.2 us; the launch traced here: 44 us
  Pallas kernels  43.2 us (98%)
  local copies, waits for them, and re-layouts  0.65 us (1%)
    pallas_call x1, Pallas kernels, make_main(): pl.pallas_call(functools.partial(main_kernel, n, total), out_shape=[shape...  34.1 us
    pallas_call x1, Pallas kernels, make_last(): pl.pallas_call(last_kernel, out_shape=jax.ShapeDtypeStruct((LANE, count *...  9.14 us

profile of v3, /device:TPU:0, one launch (start us, length us, event | category | flops | bytes accessed | tf_op | source)
XLA Modules:
  0.0 44.0 jit_solution(10352794805769934902)
XLA Ops:
  0.0 0.0 copy-start
  0.0 0.7 %copy-done = s32[128]{0:T(128)S(1)} copy-done((s32[128]{0:T(128)S(1)}, s32[128]{0:T(128)}, u32[]{:S(2)}) %copy-start) | copy-done | bytes 536
  0.7 34.1 %shard_map.37 = (bf16[512,512]{1,0:T(8,128)(2,1)S(1)}, bf16[512,512]{1,0:T(8,128)(2,1)S(1)}, bf16[512,512]{1,0:T(8,128)(2,1)S(1)}, bf16[512,512]{1,0:T(8,128)(2,...) custom-call(f32[64,4096]{1,0:T(8,128)} %source.1, ...), custom_call_target="tpu_custom_call" | custom-call | tf_op jit(solution)/shard_map/pallas_call | solution.py:318
  34.7 9.1 %shard_map.38 = f32[128,4096]{1,0:T(8,128)} custom-call(f32[128,128]{1,0:T(8,128)S(1)} %get-tuple-element.15.once, f32[256,128]{1,0:T(8,128)S(1)} %get-tuple-element.16.gram, bf16[512,512]{1,0:T(8,128)(2,1)S(1)} %get-tuple-element.17.rest_0_, bf16[512,512]{1,0:T(8,128)(2,1)S(1)} %get-tuple-element.18.rest_1_, ...), custom_call_target="tpu_custom_call" | custom-call | tf_op jit(solution)/shard_map/pallas_call | solution.py:436
Async XLA Ops:
  0.0 0.7 %copy-start = (s32[128]{0:T(128)S(1)}, s32[128]{0:T(128)}, u32[]{:S(2)}) copy-start(s32[128]{0:T(128)} %param.5) | copy-start | bytes 1540

commit v4 on v3

--- a/solution.py
+++ b/solution.py
@@ -11,6 +11,7 @@
 SUB = 8
 LANE = 128
 GROUP = 8
+PANEL = 4
 PIECE = 4 * HB
 MESH = pl.DeviceIdType.MESH
 VMEM = pl.BlockSpec(memory_space=pltpu.VMEM)
@@ -22,14 +23,23 @@
 BF16 = jnp.bfloat16
 
 
-def exact(a, b, dims=NN):
-    return lax.dot_general(
-        a, b, dims, precision=lax.Precision.HIGHEST, preferred_element_type=F32
-    )
-
-
 def bf(a, b, dims=NN):
     return lax.dot_general(a, b, dims, preferred_element_type=F32)
+
+
+def thirds(value):
+    top = value.astype(BF16)
+    rest = value - top.astype(F32)
+    middle = rest.astype(BF16)
+    return top, middle, (rest - middle.astype(F32)).astype(BF16)
+
+
+def exact(a, b, dims=NN):
+    (at,), (bt,) = dims[0]
+    a1, a2, a3 = thirds(a)
+    b1, b2, b3 = thirds(b)
+    left = jnp.concatenate([a1, a1, a2, a2, a1, a3], axis=at)
+    return bf(left, jnp.concatenate([b1, b2, b1, b2, b3, b1], axis=bt), dims)
 
 
 def halves(value):
@@ -229,9 +239,6 @@
         bands[at + 2] = band_block(bv[:, block(at)], chosen)
         return 0
 
-    loads[4].wait()
-    lax.fori_loop(0, blocks // 2, build, 0, unroll=blocks // 2)
-    loads[5].wait()
     pl.semaphore_wait(barrier, 2 + GROUP - 1 + near.groups - 1)
     near_low, near_high = pl.ds(0, HB), pl.ds(local - HB, HB)
     far_low, far_high = pl.ds(HB, deep_b), pl.ds(local - deep_s, deep_b)
@@ -249,9 +256,13 @@
         near.copy(src, dst, hsend.at[index], hrecv.at[index], target)
         for index, (src, dst, target) in enumerate(moves)
     ]
-    for copy in halo:
+    for copy in halo[:4]:
         copy.start()
-    lax.fori_loop(blocks // 2, blocks, build, 0, unroll=blocks // 2)
+    loads[4].wait()
+    loads[5].wait()
+    for copy in halo[4:]:
+        copy.start()
+    lax.fori_loop(0, blocks, build, 0, unroll=blocks)
     apply_band(bands, 0, z0, z1, True, 3, blocks - 2)
 
     def edge_source(k):
@@ -348,46 +359,74 @@
     return jnp.broadcast_to(value, (SUB, LANE))
 
 
+def outer(rows):
+    a, b, c = thirds(rows)
+    left = jnp.concatenate([part[:, :LANE] for part in (a, a, b, b, a, c)], axis=0)
+    return bf(left, jnp.concatenate([a, b, a, b, c, a], axis=0), TN)
+
+
+def column(value, k):
+    return splat(value[:, k : k + 1])
+
+
 def eliminate(metric, right):
     tiles = metric.shape[0] // SUB
-    part = [slice(SUB * t, SUB * t + SUB) for t in range(tiles)]
-    state = [[metric[part[t]], right[part[t]]] for t in range(tiles)]
+    state = [
+        [metric[SUB * t : SUB * t + SUB], right[SUB * t : SUB * t + SUB]] for t in range(tiles)
+    ]
     rows = lax.broadcasted_iota(jnp.int32, (SUB, LANE), 0)
-    solved = []
     steps = range(SUB)
+    columns = [column(state[0][0], k) for k in steps]
+    done = []
     for t0 in range(tiles):
         at = SUB * t0
-        core = {
-            (i, k): splat(state[t0][0][i : i + 1, at + k : at + k + 1])
-            for i in steps
-            for k in range(i, SUB)
-        }
-        pivots = [[splat(half[i : i + 1]) for half in state[t0]] for i in steps]
-        inverse = []
+        if t0 + 1 < tiles:
+            ahead = state[t0 + 1][0]
+            raw = [column(ahead, at + k) for k in steps]
+            following = [column(ahead, at + SUB + k) for k in steps]
+        core, inverse, pivots = {}, [], []
+        roots = jnp.ones((SUB, LANE), F32)
         for i in steps:
+            for k in range(i, SUB):
+                core[i, k] = splat(columns[k][i : i + 1])
             inverse.append(1.0 / core[i, i])
-            for k in range(i + 1, SUB):
-                ratio = core[i, k] * inverse[i]
-                for m in range(k, SUB):
-                    core[k, m] = core[k, m] - ratio * core[i, m]
-                pivots[k] = [p - ratio * q for p, q in zip(pivots[k], pivots[i])]
-        result = jnp.zeros((SUB, LANE), F32)
-        for i in steps:
-            result = jnp.where(rows == i, pivots[i][1] * lax.rsqrt(core[i, i]), result)
-        solved.append(result)
-        for t in range(t0 + 1, tiles):
-            scaled = []
+            roots = jnp.where(rows == i, lax.rsqrt(core[i, i]), roots)
+            pivots.append([splat(half[i : i + 1]) for half in state[t0]])
+            if i < SUB - 1:
+                below = jnp.where(rows > i, columns[i], 0.0)
+                for k in range(i + 1, SUB):
+                    columns[k] = columns[k] - (below * core[i, k]) * inverse[i]
+                ratio = below * inverse[i]
+                state[t0] = [half - ratio * p for half, p in zip(state[t0], pivots[i])]
+        done.append([half * roots for half in state[t0]])
+        limit = min(tiles, PANEL * (t0 // PANEL + 2))
+        for t in range(t0 + 1, limit):
+            plain, scaled = [], []
             for k in steps:
-                column = splat(state[t][0][:, at + k : at + k + 1])
+                value = raw[k] if t == t0 + 1 else column(state[t][0], at + k)
                 for i in range(k):
-                    column = column - scaled[i] * core[i, k]
-                scaled.append(column * inverse[k])
+                    value = value - scaled[i] * core[i, k]
+                plain.append(value)
+                scaled.append(value * inverse[k])
+            if t == t0 + 1:
+                columns = []
+                for j in steps:
+                    value = following[j]
+                    for k in steps:
+                        value = value - scaled[k] * splat(plain[k][j : j + 1])
+                    columns.append(value)
             for half in range(2):
                 value = state[t][half]
                 for k in steps:
                     value = value - scaled[k] * pivots[k][half]
                 state[t][half] = value
-    return jnp.concatenate(solved, axis=0)
+        if (t0 + 1) % PANEL == 0 and limit < tiles:
+            panel = [jnp.concatenate(tile, axis=1) for tile in done[-PANEL:]]
+            update = outer(jnp.concatenate(panel, axis=0))
+            for t in range(limit, tiles):
+                cut = update[SUB * t : SUB * t + SUB]
+                state[t] = [state[t][0] - cut[:, :LANE], state[t][1] - cut[:, LANE:]]
+    return jnp.concatenate([tile[1] for tile in done], axis=0)
 
 
 def square_turn(spanning, grammian):

time: 44.2 us -> 38.1 us (0.86)
  Pallas kernels: 43.2 us -> 37.1 us
    pallas_call x1, Pallas kernels: 34.1 us -> 30.7 us  [make_main(): pl.pallas_call(functools.partial(main_kernel, n, total), out_shape=[shape...]
    pallas_call x1, Pallas kernels: 9.14 us -> 6.4 us  [make_last(): pl.pallas_call(last_kernel, out_shape=jax.ShapeDtypeStruct((LANE, count *...]
where the time goes in v4:
time: 38.1 us; the launch traced here: 37.9 us
  Pallas kernels  37.1 us (97%)
  local copies, waits for them, and re-layouts  0.65 us (2%)
    pallas_call x1, Pallas kernels, make_main(): pl.pallas_call(functools.partial(main_kernel, n, total), out_shape=[shape...  30.7 us
    pallas_call x1, Pallas kernels, make_last(): pl.pallas_call(last_kernel, out_shape=jax.ShapeDtypeStruct((LANE, count *...  6.4 us

profile of v4, /device:TPU:0, one launch (start us, length us, event | category | flops | bytes accessed | tf_op | source)
XLA Modules:
  0.0 37.9 jit_solution(16656775780447353200)
XLA Ops:
  0.0 0.0 copy-start
  0.0 0.7 %copy-done = s32[128]{0:T(128)S(1)} copy-done((s32[128]{0:T(128)S(1)}, s32[128]{0:T(128)}, u32[]{:S(2)}) %copy-start) | copy-done | bytes 536
  0.7 30.7 %shard_map.37 = (bf16[512,512]{1,0:T(8,128)(2,1)S(1)}, bf16[512,512]{1,0:T(8,128)(2,1)S(1)}, bf16[512,512]{1,0:T(8,128)(2,1)S(1)}, bf16[512,512]{1,0:T(8,128)(2,...) custom-call(f32[64,4096]{1,0:T(8,128)} %source.1, ...), custom_call_target="tpu_custom_call" | custom-call | tf_op jit(solution)/shard_map/pallas_call | solution.py:329
  31.4 6.4 %shard_map.38 = f32[128,4096]{1,0:T(8,128)} custom-call(f32[128,128]{1,0:T(8,128)S(1)} %get-tuple-element.15.once, f32[256,128]{1,0:T(8,128)S(1)} %get-tuple-element.16.gram, bf16[512,512]{1,0:T(8,128)(2,1)S(1)} %get-tuple-element.17.rest_0_, bf16[512,512]{1,0:T(8,128)(2,1)S(1)} %get-tuple-element.18.rest_1_, ...), custom_call_target="tpu_custom_call" | custom-call | tf_op jit(solution)/shard_map/pallas_call | solution.py:475
Async XLA Ops:
  0.0 0.7 %copy-start = (s32[128]{0:T(128)S(1)}, s32[128]{0:T(128)}, u32[]{:S(2)}) copy-start(s32[128]{0:T(128)} %param.5) | copy-start | bytes 1540

commit v5 on v4

--- a/solution.py
+++ b/solution.py
@@ -272,13 +272,19 @@
         part_high = jnp.where(me < n - 1, hs[:, pl.ds(k * HB, HB)], 0.0)
         z0[pl.ds(3 * HB + local + k * HB, HB)] = pack_columns(part_high)
 
+    def gram_part(*parts):
+        even = jnp.concatenate([z0[pl.ds(at * HB + 3 * HB, size * HB)] for at, size in parts], axis=0)
+        odd = jnp.concatenate([z1[pl.ds(at * HB + 2 * HB, size * HB)] for at, size in parts], axis=0)
+        high, low = mixed(even, odd)
+        return bf(high, jnp.concatenate([high, low], axis=1), TN)
+
+    product = gram_part((1, blocks - 2))
     for copy in halo[:2]:
         copy.wait_recv()
     edge_source(2)
     apply_band(bands, 0, z0, z1, True, 2, 1)
     apply_band(bands, 0, z0, z1, True, blocks + 1, 1)
-    high, low = mixed(z0[pl.ds(3 * HB, local)], z1[pl.ds(2 * HB, local)])
-    product = bf(high, jnp.concatenate([high, low], axis=1), TN)
+    product = product + gram_part((0, 1), (blocks - 1, 1))
     cross = swap(product[:, LANE:])
     near.scatter(product[:, :LANE] + cross + cross.T)
 
@@ -310,9 +316,12 @@
     near.post()
     far.middle()
     gram_one = near.finish() * (1.0 / total)
-    turned = square_turn(gram_one, gram_one)
+    cube = exact(exact(gram_one, gram_one), gram_one)
+    turned = eliminate(cube, gram_one)
     far.post()
-    once[...] = square_turn(exact(turned, gram_one), gram_one)
+    spanning = exact(turned, gram_one)
+    metric = exact(exact(spanning, gram_one), spanning, NT)
+    once[...] = eliminate(metric, spanning)
     gram[...] = far.finish() * (1.0 / total)
     for copy in halo:
         copy.wait_send()
@@ -429,10 +438,6 @@
     return jnp.concatenate([tile[1] for tile in done], axis=0)
 
 
-def square_turn(spanning, grammian):
-    return eliminate(exact(exact(spanning, grammian), spanning, NT), spanning)
-
-
 def last_kernel(once, gram, *rest):
     *packs, out, tile, sem = rest
     keep = LANE
@@ -449,8 +454,7 @@
     next_b = exact(span_a, cross) + exact(span_b, far)
     metric = exact(next_a, span_a, NT) + exact(next_b, span_b, NT)
     spanning = jnp.concatenate([exact(span_a, coeffs), exact(span_b, coeffs)], axis=1)
-    coeffs = exact(eliminate(metric, unit), spanning)
-    turned = coeffs.T
+    turned = exact(spanning.T, eliminate(metric, unit), NT)
     half = LANE // 2
     weights = jnp.concatenate(halves(turned), axis=1)
     weights = jnp.concatenate(

time: 38.1 us -> 38 us (level)
  no operation moved by 1% of the time
where the time goes in v5:
time: 38 us; the launch traced here: 37.9 us
  Pallas kernels  37.1 us (98%)
  local copies, waits for them, and re-layouts  0.65 us (2%)
    pallas_call x1, Pallas kernels, make_main(): pl.pallas_call(functools.partial(main_kernel, n, total), out_shape=[shape...  30.7 us
    pallas_call x1, Pallas kernels, make_last(): pl.pallas_call(last_kernel, out_shape=jax.ShapeDtypeStruct((LANE, count *...  6.39 us

profile of v5, /device:TPU:0, one launch (start us, length us, event | category | flops | bytes accessed | tf_op | source)
XLA Modules:
  0.0 37.9 jit_solution(7203148908836770662)
XLA Ops:
  0.0 0.0 copy-start
  0.0 0.7 %copy-done = s32[128]{0:T(128)S(1)} copy-done((s32[128]{0:T(128)S(1)}, s32[128]{0:T(128)}, u32[]{:S(2)}) %copy-start) | copy-done | bytes 536
  0.7 30.7 %shard_map.37 = (bf16[512,512]{1,0:T(8,128)(2,1)S(1)}, bf16[512,512]{1,0:T(8,128)(2,1)S(1)}, bf16[512,512]{1,0:T(8,128)(2,1)S(1)}, bf16[512,512]{1,0:T(8,128)(2,...) custom-call(f32[64,4096]{1,0:T(8,128)} %source.1, ...), custom_call_target="tpu_custom_call" | custom-call | tf_op jit(solution)/shard_map/pallas_call | solution.py:338
  31.3 6.4 %shard_map.38 = f32[128,4096]{1,0:T(8,128)} custom-call(f32[128,128]{1,0:T(8,128)S(1)} %get-tuple-element.15.once, f32[256,128]{1,0:T(8,128)S(1)} %get-tuple-element.16.gram, bf16[512,512]{1,0:T(8,128)(2,1)S(1)} %get-tuple-element.17.rest_0_, bf16[512,512]{1,0:T(8,128)(2,1)S(1)} %get-tuple-element.18.rest_1_, ...), custom_call_target="tpu_custom_call" | custom-call | tf_op jit(solution)/shard_map/pallas_call | solution.py:479
Async XLA Ops:
  0.0 0.7 %copy-start = (s32[128]{0:T(128)S(1)}, s32[128]{0:T(128)}, u32[]{:S(2)}) copy-start(s32[128]{0:T(128)} %param.5) | copy-start | bytes 1540

commit v6 on v5

--- a/solution.py
+++ b/solution.py
@@ -189,8 +189,8 @@
      local_sem, hsend, hrecv, *totals) = rest[pieces + 2 :]
     me = lax.axis_index("rows")
     right, left = lax.rem(me + 1, n), lax.rem(me + n - 1, n)
-    near = Total(n, totals[: len(totals) // 2])
-    far = Total(n, totals[len(totals) // 2 :])
+    third = len(totals) // 3
+    near, mid, far = [Total(n, totals[third * k : third * k + third]) for k in range(3)]
     local = source.shape[1]
     blocks = local // HB
     deep_s, deep_b = 3 * HB, 2 * HB
@@ -299,30 +299,41 @@
     apply_band(bands, 0, z0, z1, True, 0, 2)
     apply_band(bands, 0, z0, z1, True, blocks + 2, 2)
     apply_band(bands, 1, z1, z2, False, 0, blocks + 2)
+    half = LANE // 2
+    high, low = mixed(z0[pl.ds(3 * HB, local)], z1[pl.ds(2 * HB, local)])
+
+    def gram_rows(z, *others):
+        product = bf(z, jnp.concatenate([high, low, *others], axis=1), TN)
+        product = product[:half] + product[half:]
+        parts = [product[:, k * LANE : k * LANE + LANE] for k in range(2 + len(others))]
+        return [parts[0] + swap(parts[1])] + [part + swap(part) for part in parts[2:]]
+
+    inner2 = z2[pl.ds(HB, local)]
+    mid.scatter(jnp.concatenate(gram_rows(inner2, inner2), axis=0))
     near.middle()
     apply_band(bands, 2, z2, z3, True, 0, blocks)
-    high, low = mixed(z0[pl.ds(3 * HB, local)], z1[pl.ds(2 * HB, local)])
-    high2, low2 = mixed(z2[pl.ds(HB, local)], z3[...])
-    product = bf(high2, jnp.concatenate([high, low, high2, low2], axis=1), TN)
-    other = bf(high, low2, TN)
-    cross = (product[:, :LANE] + swap(product[:, LANE : 2 * LANE])).T + swap(other)
-    own = swap(product[:, 3 * LANE :])
-    own = product[:, 2 * LANE : 3 * LANE] + own + own.T
-    far.scatter(jnp.concatenate([cross, own], axis=0))
+    inner3 = z3[...]
+    cross, left_part, own = gram_rows(inner3, inner2, inner3)
+    lanes = lax.broadcasted_iota(jnp.int32, own.shape, 1)
+    far.scatter(jnp.concatenate([cross, jnp.where(lanes < half, left_part, own)], axis=0))
     for index, out in enumerate(packs):
         for at, z in enumerate((z0, z1, z2, z3)):
             where = pl.ds(index * PIECE + (3 - at) * HB, PIECE)
             out[:, at * LANE : (at + 1) * LANE] = z[where]
+    mid.middle()
     near.post()
     far.middle()
     gram_one = near.finish() * (1.0 / total)
+    mid.post()
     cube = exact(exact(gram_one, gram_one), gram_one)
     turned = eliminate(cube, gram_one)
     far.post()
     spanning = exact(turned, gram_one)
     metric = exact(exact(spanning, gram_one), spanning, NT)
     once[...] = eliminate(metric, spanning)
-    gram[...] = far.finish() * (1.0 / total)
+    upper = mid.finish() * (1.0 / total)
+    lower = far.finish() * (1.0 / total)
+    gram[...] = jnp.concatenate([upper[:half], lower[:half], upper[half:], lower[half:]], axis=0)
     for copy in halo:
         copy.wait_send()
 
@@ -357,7 +368,8 @@
             dma((6,)), dma((6,)), dma((6,)),
         ]
         + Total.scratch(n, LANE)
-        + Total.scratch(n, 2 * LANE),
+        + Total.scratch(n, LANE)
+        + Total.scratch(n, LANE),
         compiler_params=pltpu.CompilerParams(
             collective_id=0, has_side_effects=True, vmem_limit_bytes=49 << 20
         ),
@@ -442,11 +454,12 @@
     *packs, out, tile, sem = rest
     keep = LANE
     coeffs = once[...]
-    cross, far = gram[:keep], gram[keep:]
-    cross = exact(exact(coeffs, cross), coeffs, NT)
-    far = exact(exact(coeffs, far), coeffs, NT)
     across = lax.broadcasted_iota(jnp.int32, (keep, keep), 1)
     down = lax.broadcasted_iota(jnp.int32, (keep, keep), 0)
+    cross, far = gram[:keep], gram[keep:]
+    far = jnp.where((across >= keep // 2) & (down < keep // 2), far.T, far)
+    cross = exact(exact(coeffs, cross, NT), coeffs, NT)
+    far = exact(exact(coeffs, far), coeffs, NT)
     unit = jnp.where(across == down, 1.0, 0.0)
     span_a = unit + exact(cross, cross, NT)
     span_b = cross + exact(cross, far)

time: 38 us -> 38.4 us (1.011)
  Pallas kernels: 37.1 us -> 37.5 us
where the time goes in v6:
time: 38.4 us; the launch traced here: 38.3 us
  Pallas kernels  37.5 us (98%)
  local copies, waits for them, and re-layouts  0.65 us (2%)
    pallas_call x1, Pallas kernels, make_main(): pl.pallas_call(functools.partial(main_kernel, n, total), out_shape=[shape...  30.9 us
    pallas_call x1, Pallas kernels, make_last(): pl.pallas_call(last_kernel, out_shape=jax.ShapeDtypeStruct((LANE, count *...  6.59 us

profile of v6, /device:TPU:0, one launch (start us, length us, event | category | flops | bytes accessed | tf_op | source)
XLA Modules:
  0.0 38.3 jit_solution(5497897583194491876)
XLA Ops:
  0.0 0.0 copy-start
  0.0 0.7 %copy-done = s32[128]{0:T(128)S(1)} copy-done((s32[128]{0:T(128)S(1)}, s32[128]{0:T(128)}, u32[]{:S(2)}) %copy-start) | copy-done | bytes 536
  0.7 30.9 %shard_map.37 = (bf16[512,512]{1,0:T(8,128)(2,1)S(1)}, bf16[512,512]{1,0:T(8,128)(2,1)S(1)}, bf16[512,512]{1,0:T(8,128)(2,1)S(1)}, bf16[512,512]{1,0:T(8,128)(2,...) custom-call(f32[64,4096]{1,0:T(8,128)} %source.1, ...), custom_call_target="tpu_custom_call" | custom-call | tf_op jit(solution)/shard_map/pallas_call | solution.py:349
  31.5 6.6 %shard_map.38 = f32[128,4096]{1,0:T(8,128)} custom-call(f32[128,128]{1,0:T(8,128)S(1)} %get-tuple-element.15.once, f32[256,128]{1,0:T(8,128)S(1)} %get-tuple-element.16.gram, bf16[512,512]{1,0:T(8,128)(2,1)S(1)} %get-tuple-element.17.rest_0_, bf16[512,512]{1,0:T(8,128)(2,1)S(1)} %get-tuple-element.18.rest_1_, ...), custom_call_target="tpu_custom_call" | custom-call | tf_op jit(solution)/shard_map/pallas_call | solution.py:492
Async XLA Ops:
  0.0 0.7 %copy-start = (s32[128]{0:T(128)S(1)}, s32[128]{0:T(128)}, u32[]{:S(2)}) copy-start(s32[128]{0:T(128)} %param.5) | copy-start | bytes 1540
